TPU v7x, 32 devices: a whole 2x2x4 slice. The times are simulated.
32 devices in a mesh: dp: 8 (over z, y), tp: 4 (over x, core).
Axes of the slice: x: 2, y: 2, z: 4, core: 2. Of those that a mesh axis runs over, the one named last changes fastest.
Arguments:
- node_lat: bfloat16 [16, 1885, 128], P('dp', None, 'tp')
- edge_lat: bfloat16 [16, 10910, 128], P('dp', None, 'tp')
- senders: int32 [10910], replicated
- receivers: int32 [10910], replicated
- grad_node: bfloat16 [16, 1885, 128], P('dp', None, 'tp')
- grad_edge: bfloat16 [16, 10910, 128], P('dp', None, 'tp')
- edge_w1: bfloat16 [2, 3, 128, 128], P(None, None, 'tp')
- edge_b1: float32 [2, 128], replicated
- edge_w2: bfloat16 [2, 128, 128], P(None, None, 'tp')
- edge_vec: float32 [2, 3, 128], P(None, None, 'tp')
- node_w1: bfloat16 [2, 2, 128, 128], P(None, None, 'tp')
- node_b1: float32 [2, 128], replicated
- node_w2: bfloat16 [2, 128, 128], P(None, None, 'tp')
- node_vec: float32 [2, 3, 128], P(None, None, 'tp')
Outputs:
- output 1: bfloat16 [16, 1885, 128], P('dp', None, 'tp')
- output 2: bfloat16 [16, 10910, 128], P('dp', None, 'tp')
- output 3: bfloat16 [16, 1885, 128], P('dp', None, 'tp')
- output 4: bfloat16 [16, 10910, 128], P('dp', None, 'tp')
- output 5: float32 [2, 3, 128, 128], P(None, None, 'tp')
- output 6: float32 [2, 128], replicated
- output 7: float32 [2, 128, 128], P(None, None, 'tp')
- output 8: float32 [2, 3, 128], P(None, None, 'tp')
- output 9: float32 [2, 2, 128, 128], P(None, None, 'tp')
- output 10: float32 [2, 128], replicated
- output 11: float32 [2, 128, 128], P(None, None, 'tp')
- output 12: float32 [2, 3, 128], P(None, None, 'tp')
All inputs are finite; a program needn't handle non-finite values.
Results may differ from a plain program's by a relative error of at most 0.0186387.
Values sent between devices are 32-bit elements.
A program may use at most 1 GiB of HBM per device.

v0:
```python
import jax
import jax.numpy as jnp
from jax import lax
from jax.experimental import pallas as pl
from jax.experimental.pallas import tpu as pltpu
from jax.sharding import PartitionSpec as P

LN_EPS = 1e-5
D = 128
T = 256
TN = 384
EC = 512
KS = 1408
BF = jnp.bfloat16
F32 = jnp.float32
I16 = jnp.int16
MESH = pl.DeviceIdType.MESH
VM = pl.BlockSpec(memory_space=pltpu.VMEM)
HB = pl.BlockSpec(memory_space=pl.ANY)
RESULT = pltpu.VMEM
GROUP = 4
BOTH = (0, 1)
THREE = (0, 1, 2)
OTHERS = (1, 2, 3)
EDGE_IN, GRAD_IN, EDGE_OUT, GRAD_OUT = range(4)
SEND_ORDER = (2, 3, 1)
LROWS = 7 * (D // 4)
HEAD = 16
LEADER = GROUP - 1
FINISH_SEMS = 40
VMEM_LIMIT = 63_000_000
SLABS = 8
EARLY = 6
VEC_SLAB = 5
EDGE_SLABS = (0, 1, 6, 7)
STAGES = (slice(0, EARLY), slice(EARLY, SLABS))


def dot(a, b):
    return jnp.dot(a, b, preferred_element_type=F32)


def dot_nt(a, b):
    return lax.dot_general(a, b, (((1,), (1,)), ((), ())), preferred_element_type=F32)


def mat(k, n=1):
    return slice(k * D, (k + n) * D)


def rows_of(d):
    q = D // 4
    return slice(d * q, (d + 1) * q)


def at(step, width):
    return pl.ds(pl.multiple_of(step * width, width), width)


def loop(stop, body, start=0):
    def step(j, carry):
        body(j)
        return carry

    lax.fori_loop(start, stop, step, 0)


def column_sum(val):
    return jnp.sum(val, axis=0, keepdims=True)


def flip(val):
    return jnp.swapaxes(val, 0, 1)


def stacked(parts):
    return jnp.concatenate(parts, axis=0)


def beside(parts):
    return jnp.concatenate(parts, axis=1)


def slot(d):
    return d - 1


def sigmoid(hidden):
    return 1.0 / (1.0 + jnp.exp(-hidden))


def fold(val):
    total = val[:, mat(0)]
    for start in range(D, val.shape[1], D):
        total = total + val[:, start:start + D]
    return total


def swap_halves(val):
    return stacked([val[rows_of(d)] for d in (1, 0, 3, 2)])


def gather(table, keys, iota):
    acc = None
    nodes = table.shape[1]
    one, zero = jnp.ones((), BF), jnp.zeros((), BF)
    for base in range(0, nodes, T):
        width = min(T, nodes - base)
        ids = iota[0:width, :]
        hot = beside([jnp.where(ids == (key - jnp.asarray(base, I16)), one, zero) for key in keys])
        part = dot(table[:, base:base + width], hot)
        acc = part if acc is None else acc + part
    return acc


def scatter(acc_ref, val, cols, lanes):
    nodes = acc_ref.shape[1]
    one, zero = jnp.ones((), BF), jnp.zeros((), BF)
    row = lanes[0:1, :]
    for base in range(0, nodes, T):
        width = min(T, nodes - base)
        hot = beside([jnp.where((row + jnp.asarray(base + s, I16)) == cols, one, zero) for s in range(0, width, D)])
        acc_ref[:, base:base + width] += dot(val, hot)


def mlp_tail(hidden, w2t, vec):
    act = (hidden * sigmoid(hidden)).astype(BF)
    out = dot(w2t, act) + vec[0]
    mean = column_sum(out) / D
    centered = out - mean
    var = column_sum(centered * centered) / D
    inv = lax.rsqrt(var + LN_EPS)
    normed = centered * inv
    message = (normed * vec[1] + vec[2]).astype(BF)
    return message, normed, inv


def mlp_back(d_msg, hidden, normed, inv, w2, vec):
    d_normed = d_msg * vec[1]
    mean0 = column_sum(d_normed) / D
    mean1 = column_sum(d_normed * normed) / D
    d_out = inv * (d_normed - mean0 - normed * mean1)
    d_out_bf = d_out.astype(BF)
    sig = sigmoid(hidden)
    act = (hidden * sig).astype(BF)
    d_w2 = dot_nt(d_out_bf, act)
    d_hidden = dot(w2, d_out_bf) * (sig * (1.0 + hidden * (1.0 - sig)))
    sums = (fold(d_out), fold(d_msg * normed), fold(d_msg), fold(d_hidden))
    return d_hidden.astype(BF), d_w2, sums


def add_sums(ref, parts):
    for q in range(4):
        total = parts[0][q]
        for other in parts[1:]:
            total = total + other[q]
        ref[mat(q), :] += total


def step_kernel(dims, *refs):
    layers, cols, nodes, edges, npad, eh, dpn = dims
    nch = eh // EC
    top = layers - 1
    n_in = 14
    hbm_in = refs[:n_in]
    n_out = 12
    (node_raw, edge_raw, gnode_raw, gedge_raw, ew1_buf, eb1_buf, ew2_buf, evec_buf, nw1_buf, nb1_buf, nw2_buf, nvec_buf) = refs[n_in:n_in + n_out]
    (send_ids, recv_ids, ew1_in, ew2_in, nw1_in, nw2_in, evec_in, nvec_in, eb1_in, nb1_in, w_send, w_recv, n_send, n_recv, gn_send, gn_recv, no_send, no_recv, dn_send, dn_recv,
     e_send, g_send, e_recv, g_recv, eo_recv, de_recv, part, part_recv, hidden, normed, inv, nhid, nnrm, ninv, d_part, s_sum, r_sum,
     ids_raw, bias_cols, sums, grad, core_recv, half, dp_recv, cross_send, cross_recv, own_sum, gathered,
     core_ss, core_rs, dp_ss, dp_rs, cross_ss, cross_rs, load_sem, w_ss, w_rs, n_ss, n_rs, e_ss, e_rs, o_rs, p_ss, p_rs, ready) = refs[n_in + n_out:]

    t = lax.axis_index('tp')
    p = lax.axis_index('dp')
    per = SLABS // dpn
    dp_others = range(1, dpn)
    x, c = t // 2, lax.rem(t, 2)
    ox, oc = 1 - x, 1 - c
    peer = [t, t + 1 - 2 * c, t + 2 - 4 * x, t + 3 - 2 * c - 4 * x]

    def remote(src, dst, ssem, rsem, d):
        return pltpu.make_async_remote_copy(src_ref=src, dst_ref=dst, send_sem=ssem, recv_sem=rsem,
                                            device_id={'tp': peer[d]}, device_id_type=MESH)

    small_in = (send_ids, recv_ids, ew1_in, ew2_in, nw1_in, nw2_in, evec_in, nvec_in, eb1_in, nb1_in)
    loads = [pltpu.make_async_copy(src, dst, load_sem.at[q]) for q, (src, dst) in enumerate(
        zip(hbm_in, (node_raw, edge_raw, gnode_raw, gedge_raw) + small_in))]

    def node_copies(send, recv, kind):
        return (remote(send.at[1], recv.at[0], n_ss.at[kind, 0], n_rs.at[kind, 0], 1),
                remote(send.at[0], recv.at[1], n_ss.at[kind, 1], n_rs.at[kind, 1], 2),
                remote(recv.at[1], recv.at[2], n_ss.at[kind, 2], n_rs.at[kind, 2], 1))

    piece = w_send.shape[0] // dpn

    def packed(l, k, count=1):
        return pl.ds(HEAD + l * LROWS + k * cols, count * cols)

    def weight_rows(owner):
        return pl.ds(pl.multiple_of(owner * piece, 8), piece)

    w_pair = remote(w_send, w_recv.at[0], w_ss.at[0], w_rs.at[0], 1)
    w_cross = remote(w_send.at[weight_rows(p)], w_recv.at[1, weight_rows(p)], w_ss.at[1], w_rs.at[1], 2)
    w_relay = remote(w_recv.at[1], w_recv.at[2], w_ss.at[2], w_rs.at[2], 1)

    def weight_copy(i, owner):
        rows = w_recv.at[1, weight_rows(owner)]
        return dp_remote(rows, rows, 2, 0, i)

    last = nch - 1
    hold = nch - 3
    buffers = ((e_send, e_recv), (g_send, g_recv), (e_send, eo_recv), (g_send, de_recv))

    def outward(kind):
        return kind in (EDGE_OUT, GRAD_OUT)

    def edge_part(kind, index, send_sem, recv_sem, d):
        src, dst = buffers[kind]
        recv_sems = o_rs.at[kind - EDGE_OUT, recv_sem] if outward(kind) else e_rs.at[kind, recv_sem]
        return remote(src.at[index], dst.at[index], e_ss.at[kind, send_sem], recv_sems, d)

    def by_half(half_id, j, action):
        narrow = jnp.logical_and(j == last, half_id == 1)

        @pl.when(jnp.logical_not(narrow))
        def _():
            action(slice(None))

        @pl.when(narrow)
        def _():
            action(slice(T))

    def edge_start(kind, j, d):
        other = oc if d % 2 else c
        if outward(kind):
            send_sem, recv_sem = jnp.where(j == last, 1, 0), jnp.where(j == last, 2 + slot(d), jnp.where(j < hold, 0, 1))
        else:
            send_sem, recv_sem = jnp.where(j == last, d, 0), j
        by_half(c if outward(kind) else other, j,
                lambda used: edge_part(kind, (slot(d), j, slice(None), used), send_sem, recv_sem, d).start())

    def edges_sent(kind):
        every = slice(None)
        edge_part(kind, (every, slice(0, last)), 0, 0, 1).wait_send()
        if outward(kind):
            by_half(c, last, lambda used: edge_part(kind, (every, last, every, used), 1, 0, 1).wait_send())
        else:
            for d in OTHERS:
                by_half(oc if d % 2 else c, last, lambda used: edge_part(kind, (slot(d), last, every, used), d, 0, d).wait_send())

    def chunk_arrived(kind, j):
        every = slice(None)
        by_half(c, j, lambda used: edge_part(kind, (every, j, every, used), 0, j, 1).wait_recv())

    def group_arrived(kind, group):
        every = slice(None)
        if group < 2:
            edge_part(kind, (every, (slice(0, hold), slice(hold, last))[group]), 0, group, 1).wait_recv()
        else:
            for d in OTHERS:
                by_half(oc if d % 2 else c, last, lambda used: edge_part(kind, (slot(d), last, every, used), 0, 2 + slot(d), d).wait_recv())

    def core_copy(l, b, stage):
        first, count = ((0, EARLY), (EARLY, SLABS - EARLY))[stage]
        return remote(grad.at[l, pl.ds(first, count), pl.ds((2 * b + 1) * cols, cols), :], core_recv.at[l, b, pl.ds(first, count)],
                      core_ss.at[l, stage], core_rs.at[l, stage], 1)

    def core_all(l, stage):
        part_of = core_recv.at[l, :, (slice(0, EARLY), slice(EARLY, SLABS))[stage]]
        return remote(part_of, part_of, core_ss.at[l, stage], core_rs.at[l, stage], 1)

    def seat(device):
        return lax.rem(device + dpn // 2, dpn)

    def in_stage(device, stage):
        early = (seat(device) + 1) * per <= EARLY
        return jnp.logical_not(early) if stage else early

    def dp_remote(src, dst, stage, l, i):
        return pltpu.make_async_remote_copy(src_ref=src, dst_ref=dst, send_sem=dp_ss.at[stage, l], recv_sem=dp_rs.at[stage, l],
                                            device_id={'dp': lax.rem(p + i, dpn)}, device_id_type=MESH)

    def spread_copy(l, i):
        return dp_remote(half.at[l, pl.ds(seat(lax.rem(p + i, dpn)) * per, per)], dp_recv.at[l, pl.ds((i - 1) * per, per)], 0, l, i)

    def dp_all(l, stage):
        most = (dpn - 1) * per
        part_of = (dp_recv.at[l], gathered.at[l, pl.ds(0, most)], w_recv.at[1, pl.ds(0, (dpn - 1) * piece)])[stage]
        return dp_remote(part_of, part_of, stage, l, 1)

    def cross_copy(l):
        return remote(cross_send.at[l], cross_recv.at[l], cross_ss.at[l], cross_rs.at[l], 2)

    def gather_copy(l, i, owner):
        return dp_remote(own_sum.at[l], gathered.at[l, pl.ds(seat(owner) * per, per)], 1, l, i)

    def part_copy(q):
        return remote(part.at[q], part_recv.at[q], p_ss.at[q], p_rs.at[q], 1)

    def load_nodes(raw, send, own):
        send[...] = jnp.zeros_like(send)
        send[0, :, :nodes] = raw[ox].astype(F32)
        send[1, :, :nodes] = raw[x].astype(F32)
        own[:cols, :] = send[1].astype(own.dtype)

    def load_edges(raw, send, own, kind):
        def put(j, lanes_j, val_of):
            for d in OTHERS:
                sample = x if d < 2 else ox
                send[slot(d), j] = val_of(sample, oc if d % 2 else c).astype(F32)
            own[:cols, lanes_j] = val_of(x, c)

        def chunk(j):
            put(j, at(j, EC), lambda s, h: raw[s, :, pl.ds(pl.multiple_of(h * eh + j * EC, D), EC)])
            for d in SEND_ORDER:
                edge_start(kind, j, d)

        loop(nch - 1, chunk)
        first = (nch - 1) * EC
        used = edges - eh - first
        last = pl.ds(first, EC)

        def tail(s, h):
            left = raw[s, :, pl.ds(first, EC)]
            right = beside([raw[s, :, pl.ds(eh + first, used)], jnp.zeros((cols, EC - used), BF)])
            return jnp.where(h == 0, left.astype(F32), right.astype(F32)).astype(BF)

        put(nch - 1, last, tail)
        for d in SEND_ORDER:
            edge_start(kind, nch - 1, d)

    def place_edges(raw, block, d, j):
        s = x if d < 2 else ox
        h = oc if d % 2 else c
        val = block.astype(BF)
        first = (nch - 1) * EC
        used = edges - eh - first

        @pl.when(jnp.logical_or(j < nch - 1, h == 0))
        def _():
            raw[s, :, pl.ds(pl.multiple_of(h * eh + j * EC, D), EC)] = val

        @pl.when(jnp.logical_and(j == nch - 1, h == 1))
        def _():
            raw[s, :, pl.ds(eh + first, used)] = val[:, :used]

    def scoped(e0, e1, ge, msg, v0, v1, v2, agg0, agg1, d_agg, scol, rcol, srow, rrow, iota, lanes, ew1, ew1t, ew2, ew2t, nw1, nw1t, nw2, nw2t, vecs):
        tables = (v0, v1, v2)
        aggs = (agg0, agg1)
        edges_in = (e0, e1)

        barrier = pltpu.get_barrier_semaphore()
        for d in OTHERS:
            pl.semaphore_signal(barrier, inc=1, device_id={'tp': peer[d]}, device_id_type=MESH)
        for copy in loads[:1] + loads[4:] + loads[1:4]:
            copy.start()
        loads[0].wait()
        with jax.named_scope('send_nodes'):
            load_nodes(node_raw, n_send, v0)
        ncop = node_copies(n_send, n_recv, 0)
        for copy in loads[4:]:
            copy.wait()
        q = cols
        w_send[:HEAD, :] = jnp.zeros((HEAD, D), F32)
        for k in THREE:
            w_send[k * layers:(k + 1) * layers, :cols] = evec_in[k]
            w_send[(3 + k) * layers:(4 + k) * layers, :cols] = nvec_in[k]
        for l in range(layers):
            w_send[packed(l, 0, 3), :] = ew1_in[pl.ds(l * 3 * q, 3 * q), :].astype(F32)
            w_send[packed(l, 3), :] = ew2_in[pl.ds(l * q, q), :].astype(F32)
            w_send[packed(l, 4, 2), :] = nw1_in[pl.ds(l * 2 * q, 2 * q), :].astype(F32)
            w_send[packed(l, 6), :] = nw2_in[pl.ds(l * q, q), :].astype(F32)
        with jax.named_scope('barrier'):
            @pl.when(t != LEADER)
            def _():
                pl.semaphore_wait(barrier, len(OTHERS))
                pl.semaphore_signal(ready, inc=1, device_id={'tp': LEADER}, device_id_type=MESH)

            @pl.when(t == LEADER)
            def _():
                pl.semaphore_wait(ready, len(OTHERS))
                for i in dp_others:
                    pl.semaphore_signal(barrier, inc=1, device_id={'dp': lax.rem(p + i, dpn)}, device_id_type=MESH)

        w_cross.start()
        w_pair.start()
        ncop[1].start()
        ncop[0].start()
        loads[1].wait()
        with jax.named_scope('send_edges'):
            load_edges(edge_raw, e_send, e0, EDGE_IN)
        loads[2].wait()
        load_nodes(gnode_raw, gn_send, d_part)
        gcop = node_copies(gn_send, gn_recv, 1)
        gcop[1].start()
        gcop[0].start()
        loads[3].wait()
        with jax.named_scope('send_grads'):
            load_edges(gedge_raw, g_send, ge, GRAD_IN)

        with jax.named_scope('dp_barrier'):
            @pl.when(t == LEADER)
            def _():
                pl.semaphore_wait(barrier, len(OTHERS) + dpn - 1)
                for d in OTHERS:
                    pl.semaphore_signal(ready, inc=1, device_id={'tp': peer[d]}, device_id_type=MESH)

            @pl.when(t != LEADER)
            def _():
                pl.semaphore_wait(ready, 1)

        w_cross.wait_recv()
        for i in dp_others:
            weight_copy(i, p).start()

        @pl.when(c == 1)
        def _():
            for recv in (e_recv, g_recv):
                recv[:, nch - 1, :, T:] = jnp.zeros((3, cols, EC - T), F32)

        iota[...] = lax.broadcasted_iota(jnp.int32, (T, D), 0).astype(I16)
        lanes[...] = lax.broadcasted_iota(jnp.int32, (16, D), 1).astype(I16)

        ids_raw[...] = jnp.full(ids_raw.shape, -1, jnp.int32)
        for which, src in enumerate((send_ids, recv_ids)):
            ids_raw[which:which + 1, :edges] = src[...].reshape(1, edges)

        def ids(b):
            for which, (row_ref, col_ref) in enumerate(((srow, scol), (rrow, rcol))):
                wide = jnp.broadcast_to(ids_raw[which:which + 1, pl.ds(pl.multiple_of(c * eh + b * D, D), D)], (D, D))
                row_ref[at(b, 16), :] = wide[:16].astype(I16)
                col_ref[at(b, D), :] = flip(wide.astype(F32)).astype(jnp.int32).astype(I16)

        with jax.named_scope('ids'):
            loop(eh // D, ids)

        def keys(ref, step):
            return [ref[pl.ds(pl.multiple_of(step * (KS // D) * 16 + 16 * h, 16), 1), :] for h in range(KS // D)]

        bias_cols[...] = flip(stacked([eb1_in[...], nb1_in[...], jnp.zeros((D - 2 * layers, D), F32)]))

        def join_weights(l):
            for d in range(GROUP):
                src = w_recv.at[slot(d)] if d else w_send
                r = rows_of(d)
                for k in THREE:
                    ew1[l, pl.ds(k * D + d * q, q), :] = src[packed(l, k), :].astype(BF)
                ew2t[l, r, :] = src[packed(l, 3), :].astype(BF)
                for k in BOTH:
                    nw1[l, pl.ds(k * D + d * q, q), :] = src[packed(l, 4 + k), :].astype(BF)
                nw2t[l, r, :] = src[packed(l, 6), :].astype(BF)

            def flip_bf(mat):
                return flip(mat.astype(F32)).astype(BF)

            for k in THREE:
                ew1t[l, :, mat(k)] = flip_bf(ew1[l, mat(k), :])
            for k in BOTH:
                nw1t[l, :, mat(k)] = flip_bf(nw1[l, mat(k), :])
            ew2[l] = flip_bf(ew2t[l])
            nw2[l] = flip_bf(nw2t[l])

        def wait_recvs(copies):
            copies[1].wait_recv()
            copies[2].start()
            copies[0].wait_recv()
            copies[2].wait_recv()

        with jax.named_scope('node_wait'):
            wait_recvs(ncop)
        for d in OTHERS:
            v0[rows_of(d), :] = n_recv[slot(d)].astype(BF)
        with jax.named_scope('weight_wait'):
            dp_all(0, 2).wait_recv()
            w_relay.start()
            w_pair.wait_recv()
            w_relay.wait_recv()
        rows_all = beside([w_send[:HEAD, :cols]] + [w_recv[d, :HEAD, :cols] for d in range(3)])
        vecs[...] = flip(stacked([rows_all, jnp.zeros((D - HEAD, D), F32)]))
        join_weights(0)

        def vec(l, node):
            first = 6 * node + l
            return [vecs[:, first + 2 * k:first + 2 * k + 1] for k in THREE]

        def bias(l, node):
            return bias_cols[:, node * layers + l:node * layers + l + 1]

        def hidden_of_nodes(l):
            table, b1 = tables[l], bias(l, 0)

            def body(step):
                xs = gather(table, keys(srow, step), iota).astype(BF)
                xr = gather(table, keys(rrow, step), iota).astype(BF)
                hidden[l, :, at(step, KS)] = dot(ew1t[l, :, mat(1, 2)], stacked([xs, xr])) + b1

            loop(eh // KS, body)

        def edge_forward(l):
            e_in = edges_in[l]

            def body(j):
                for sub in range(EC // T):
                    a = at(j * (EC // T) + sub, T)
                    if l == 0:
                        if sub == 0:
                            chunk_arrived(EDGE_IN, j)
                        for d in OTHERS:
                            e_in[rows_of(d), a] = e_recv[slot(d), j, :, sub * T:(sub + 1) * T].astype(BF)
                    e_val = e_in[:, a]
                    hid = hidden[l, :, a] + dot(ew1t[l, :, mat(0)], e_val)
                    hidden[l, :, a] = hid
                    message, nrm, std = mlp_tail(hid, ew2t[l], vec(l, 0))
                    normed[l, :, a] = nrm
                    inv[l:l + 1, a] = std
                    msg[:, a] = message
                    e_new = (e_val.astype(F32) + message.astype(F32)).astype(BF)
                    if l < top:
                        edges_in[l + 1][:, a] = e_new
                    else:
                        for d in OTHERS:
                            e_send[slot(d), j, :, sub * T:(sub + 1) * T] = e_new[rows_of(d)].astype(F32)
                        if sub == 0:
                            own_parts = []
                        own_parts.append(e_new[:q])
                if l == top:
                    for d in SEND_ORDER:
                        edge_start(EDGE_OUT, j, d)
                    place_edges(edge_raw, beside(own_parts), 0, j)

            loop(nch, body)

        def segment_sum(acc, ids_ref):
            acc[...] = jnp.zeros(acc.shape, F32)

            def body(step):
                scatter(acc, msg[:, at(step, KS)], ids_ref[at(step, KS), :], lanes)

            loop(eh // KS, body)

        def node_forward(l):
            table, agg, out = tables[l], aggs[l], tables[l + 1]

            def body(step):
                a = pl.ds(pl.multiple_of(step * TN, D), TN)
                v_in = table[:, a]
                agg_bf = (part[l, :, a] + swap_halves(part_recv[l, :, a])).astype(BF)
                agg[:, a] = agg_bf
                hid = dot(nw1t[l], stacked([v_in, agg_bf])) + bias(l, 1)
                nhid[l, :, a] = hid
                message, nrm, std = mlp_tail(hid, nw2t[l], vec(l, 1))
                nnrm[l, :, a] = nrm
                ninv[l:l + 1, a] = std
                out[:, a] = (v_in.astype(F32) + message.astype(F32)).astype(BF)

            loop(npad // TN, body)

        for l in range(layers):
            with jax.named_scope(f'gather_{l}'):
                hidden_of_nodes(l)
            if l == top:
                edges_sent(EDGE_IN)
            with jax.named_scope(f'edge_forward_{l}'):
                edge_forward(l)
            with jax.named_scope(f'sum_{l}'):
                segment_sum(part.at[l], rcol)
            part_copy(l).start()
            if l == 0:
                join_weights(1)
                gcop[1].wait_recv()
                gcop[2].start()
            with jax.named_scope(f'part_wait_{l}'):
                part_copy(l).wait_recv()
            with jax.named_scope(f'node_forward_{l}'):
                node_forward(l)
        no_send[...] = tables[layers][rows_of(2), :].astype(F32)
        no_copy = remote(no_send, no_recv, n_ss.at[2, 0], n_rs.at[2, 0], 2)
        no_copy.start()
        node_raw[x] = tables[layers][:q, :nodes]

        grad[...] = jnp.zeros_like(grad)
        sums[...] = jnp.zeros_like(sums)
        with jax.named_scope('grad_node_wait'):
            gcop[0].wait_recv()
            gcop[2].wait_recv()
        for d in OTHERS:
            d_part[rows_of(d), :] = gn_recv[slot(d)]

        def node_backward(l):
            table, agg = tables[l], aggs[l]

            def body(step):
                a = pl.ds(pl.multiple_of(step * TN, D), TN)
                d_in = d_part[:, a]
                if l < top:
                    d_in = d_in + part[layers + l + 1, :, a] + swap_halves(part_recv[layers + l + 1, :, a])
                    d_in = d_in.astype(BF).astype(F32)
                d_hid, d_w2, parts = mlp_back(d_in, nhid[l, :, a], nnrm[l, :, a], ninv[l:l + 1, a], nw2[l], vec(l, 1))
                add_sums(sums.at[l, 1], [parts])
                grad[l, 4] += d_w2
                grad[l, 2] += dot_nt(table[:, a], d_hid)
                grad[l, 3] += dot_nt(agg[:, a], d_hid)
                d_part[:, a] = d_in + dot(nw1[l, mat(0), :], d_hid)
                d_agg[:, a] = dot(nw1[l, mat(1), :], d_hid).astype(BF)

            loop(npad // TN, body)

        def gather_back():
            def body(step):
                msg[:, at(step, KS)] = gather(d_agg, keys(rrow, step), iota).astype(BF)

            loop(eh // KS, body)

        def edge_backward(l):
            e_in = edges_in[l]

            def body(j):
                all_parts, d_w2s, d_w1s, own_parts = [], [], [], []
                for sub in range(EC // T):
                    a = at(j * (EC // T) + sub, T)
                    if l == top:
                        if sub == 0:
                            chunk_arrived(GRAD_IN, j)
                        for d in OTHERS:
                            ge[rows_of(d), a] = g_recv[slot(d), j, :, sub * T:(sub + 1) * T].astype(BF)
                    d_res = ge[:, a].astype(F32)
                    d_msg = d_res + msg[:, a].astype(F32)
                    d_hid, d_w2, parts = mlp_back(d_msg, hidden[l, :, a], normed[l, :, a], inv[l:l + 1, a], ew2[l], vec(l, 0))
                    all_parts.append(parts)
                    d_w2s.append(d_w2)
                    d_w1s.append(dot_nt(e_in[:, a], d_hid))
                    msg[:, a] = d_hid
                    d_new = (d_res + dot(ew1[l, mat(0), :], d_hid)).astype(BF)
                    if l > 0:
                        ge[:, a] = d_new
                    else:
                        for d in OTHERS:
                            g_send[slot(d), j, :, sub * T:(sub + 1) * T] = d_new[rows_of(d)].astype(F32)
                        own_parts.append(d_new[:q])
                add_sums(sums.at[l, 0], all_parts)
                grad[l, 1] += sum(d_w2s[1:], d_w2s[0])
                grad[l, 0] += sum(d_w1s[1:], d_w1s[0])
                if l == 0:
                    @pl.when(j < hold)
                    def _():
                        for d in SEND_ORDER:
                            edge_start(GRAD_OUT, j, d)
                    place_edges(gedge_raw, beside(own_parts), 0, j)

            loop(nch, body)

        def vector_slab(l):
            def total(node, k):
                return column_sum(flip(sums[l, node, mat(k), :]))

            lat = stacked([total(node, k) for node in BOTH for k in THREE])
            biases = stacked([total(node, 3) for node in BOTH])
            n_lat = lat.shape[0]
            for d in range(GROUP):
                grad[l, VEC_SLAB, d * cols:d * cols + n_lat, :cols] = lat[:, rows_of(d)]
                grad[l, VEC_SLAB, d * cols + n_lat:d * cols + n_lat + 2, :] = biases

        def reduce_start(l, stage):
            for b in BOTH:
                core_copy(l, b, stage).start()

        def chip_sum(l, stage):
            row = lax.broadcasted_iota(jnp.int32, (cols, D), 0)
            edge_row = jnp.logical_or(row < 3, row == 6)
            core_all(l, stage).wait_recv()
            for b in BOTH:
                for k in range(SLABS)[STAGES[stage]]:
                    own = grad[l, k, rows_of(2 * b), :]
                    if k in EDGE_SLABS:
                        own = own + core_recv[l, b, k]
                    elif k == VEC_SLAB:
                        own = own + jnp.where(edge_row, core_recv[l, b, k], 0.0)
                    half[l, k, b] = own
            for i in dp_others:
                @pl.when(in_stage(lax.rem(p + i, dpn), stage))
                def _():
                    spread_copy(l, i).start()

        def dp_sum(l, stage):
            @pl.when(in_stage(p, stage))
            def _():
                total = half[l, pl.ds(seat(p) * per, per)]
                dp_all(l, 0).wait_recv()
                for i in dp_others:
                    total = total + dp_recv[l, pl.ds((i - 1) * per, per)]
                own_sum[l] = total[:, 0]
                cross_send[l] = total[:, 1]
                cross_copy(l).start()

        def cross_sum(l):
            cross_copy(l).wait_recv()
            total = own_sum[l] + cross_recv[l]
            own_sum[l] = total
            gathered[l, pl.ds(seat(p) * per, per)] = total
            for i in dp_others:
                gather_copy(l, i, p).start()

        def project(l):
            table = tables[l]

            def body(step):
                a = pl.ds(pl.multiple_of(step * TN, D), TN)
                s_bf, r_bf, v_in = s_sum[:, a].astype(BF), r_sum[:, a].astype(BF), table[:, a]
                part[layers + l, :, a] = dot(ew1[l, mat(1), :], s_bf) + dot(ew1[l, mat(2), :], r_bf)
                grad[l, 6] += dot_nt(v_in, s_bf)
                grad[l, 7] += dot_nt(v_in, r_bf)

            loop(npad // TN, body)

        for l in reversed(range(layers)):
            first_layer = l == 0
            with jax.named_scope(f'node_backward_{l}'):
                node_backward(l)
            if first_layer:
                with jax.named_scope('chip_sum_1'):
                    chip_sum(1, 0)
                    chip_sum(1, 1)
            with jax.named_scope(f'gather_back_{l}'):
                gather_back()
            if first_layer:
                edges_sent(GRAD_IN)
            with jax.named_scope(f'edge_backward_{l}'):
                edge_backward(l)
            vector_slab(l)
            reduce_start(l, 0)
            if first_layer:
                with jax.named_scope('dp_sum_1'):
                    dp_sum(1, 0)
                    dp_sum(1, 1)
            with jax.named_scope(f'sum_send_{l}'):
                segment_sum(s_sum, scol)
            if first_layer:
                with jax.named_scope('chip_sum_0'):
                    chip_sum(0, 0)
            with jax.named_scope(f'sum_recv_{l}'):
                segment_sum(r_sum, rcol)
            with jax.named_scope(f'project_{l}'):
                project(l)
            reduce_start(l, 1)
            part_copy(layers + l).start()
            if first_layer:
                with jax.named_scope('chip_sum_late'):
                    chip_sum(0, 1)
                with jax.named_scope('dp_sum_0'):
                    dp_sum(0, 0)
            with jax.named_scope(f'back_wait_{l}'):
                part_copy(layers + l).wait_recv()

        def final(step):
            a = pl.ds(pl.multiple_of(step * TN, D), TN)
            d_in = (d_part[:, a] + part[layers, :, a] + swap_halves(part_recv[layers, :, a])).astype(BF)
            v2[:, a] = d_in

        loop(npad // TN, final)
        gnode_raw[x] = v2[:q, :nodes]
        with jax.named_scope('dp_sum_late'):
            dp_sum(0, 1)

        dn_send[...] = v2[rows_of(2), :].astype(F32)
        dn_copy = remote(dn_send, dn_recv, n_ss.at[2, 1], n_rs.at[2, 1], 2)
        dn_copy.start()

        def send_rest(j):
            for d in SEND_ORDER:
                edge_start(GRAD_OUT, j, d)

        loop(nch, send_rest, hold)

        with jax.named_scope('node_out_wait'):
            no_copy.wait_recv()
        node_raw[ox] = no_recv[:, :nodes].astype(BF)

        def place_e(j):
            for d in OTHERS:
                place_edges(edge_raw, eo_recv[slot(d), j], d, j)

        with jax.named_scope('place_edge_out'):
            for group in THREE:
                group_arrived(EDGE_OUT, group)
            loop(nch, place_e)

        def place_g(j):
            for d in OTHERS:
                place_edges(gedge_raw, de_recv[slot(d), j], d, j)

        with jax.named_scope('place_first'):
            group_arrived(GRAD_OUT, 0)
            loop(hold, place_g)
        for l in range(layers):
            with jax.named_scope(f'cross_sum_{l}'):
                cross_sum(l)
        with jax.named_scope('d_node_wait'):
            dn_copy.wait_recv()
        gnode_raw[ox] = dn_recv[:, :nodes].astype(BF)
        with jax.named_scope('place_rest'):
            group_arrived(GRAD_OUT, 1)
            loop(last, place_g, hold)
        for l in range(layers):
            dp_all(l, 1).wait_recv()
            ew1_buf[l, 0] = gathered[l, 0]
            ew1_buf[l, 1:] = gathered[l, EARLY:]
            ew2_buf[l] = gathered[l, 1]
            nw1_buf[l] = gathered[l, 2:4]
            nw2_buf[l] = gathered[l, 4]
            small = gathered[l, VEC_SLAB]
            for k in THREE:
                evec_buf[k, l:l + 1, :] = small[k:k + 1, :cols]
                nvec_buf[k, l:l + 1, :] = small[3 + k:4 + k, :cols]
            eb1_buf[l:l + 1, :] = small[6:7]
            nb1_buf[l:l + 1, :] = small[7:8]
        for l in range(layers):
            for stage in BOTH:
                core_all(l, stage).wait_send()
            cross_copy(l).wait_send()
            dp_all(l, 0).wait_send()
            dp_all(l, 1).wait_send()
        for copy in ncop + gcop + (w_pair, w_cross, w_relay):
            copy.wait_send()
        dp_all(0, 2).wait_send()
        no_copy.wait_send()
        dn_copy.wait_send()
        for k in range(2 * layers):
            part_copy(k).wait_send()
        edges_sent(EDGE_OUT)
        with jax.named_scope('place_last'):
            group_arrived(GRAD_OUT, 2)
            loop(nch, place_g, last)
        edges_sent(GRAD_OUT)

    bf = lambda *s: pltpu.VMEM(s, BF)
    pl.run_scoped(
        scoped, bf(D, eh), bf(D, eh), bf(D, eh), bf(D, eh), bf(D, npad), bf(D, npad), bf(D, npad), bf(D, npad), bf(D, npad), bf(D, npad),
        pltpu.VMEM((eh, D), I16), pltpu.VMEM((eh, D), I16), pltpu.VMEM((eh // D * 16, D), I16), pltpu.VMEM((eh // D * 16, D), I16),
        pltpu.VMEM((T, D), I16), pltpu.VMEM((16, D), I16),
        bf(layers, 3 * D, D), bf(layers, D, 3 * D), bf(layers, D, D), bf(layers, D, D),
        bf(layers, 2 * D, D), bf(layers, D, 2 * D), bf(layers, D, D), bf(layers, D, D), pltpu.VMEM((D, D), F32))


def finish_moves(src, dst):
    if len(src.shape) != 3 or src.dtype != BF:
        return [(src, dst)]
    return [(src.at[s, pl.ds(r, 8)], dst.at[s, pl.ds(r, 8)]) for s in range(src.shape[0]) for r in range(0, src.shape[1], 8)]


def finish_kernel(*refs):
    count = len(refs) // 2
    moves = sum((finish_moves(refs[k], refs[count + k]) for k in range(count)), [])
    puts = [pltpu.make_async_copy(src, dst, refs[-1].at[k]) for k, (src, dst) in enumerate(moves)]
    for put in puts:
        put.start()
    for put in puts:
        put.wait()


def keep_in_vmem(val):
    return pltpu.with_memory_space_constraint(val, pltpu.VMEM)


def finish(arrays):
    return pl.pallas_call(
        finish_kernel,
        name='finish',
        out_shape=[jax.ShapeDtypeStruct(a.shape, a.dtype) for a in arrays],
        in_specs=[VM] * len(arrays),
        out_specs=[HB] * len(arrays),
        scratch_shapes=[pltpu.SemaphoreType.DMA((FINISH_SEMS,))],
        compiler_params=pltpu.CompilerParams(vmem_limit_bytes=1 << 20),
    )(*[keep_in_vmem(a) for a in arrays])


def solution(mesh):
    lat_spec = P('dp', None, 'tp')
    first_spec = P(None, None, 'tp', None)
    col_spec = P(None, None, 'tp')
    param_specs = (first_spec, P(), col_spec, col_spec, first_spec, P(), col_spec, col_spec)
    in_specs = (lat_spec, lat_spec, P(), P(), lat_spec, lat_spec) + param_specs
    out_specs = (lat_spec, lat_spec, lat_spec, lat_spec) + param_specs
    shape = jax.ShapeDtypeStruct

    def local_step(node_lat, edge_lat, senders, receivers, grad_node, grad_edge, edge_w1, edge_b1, edge_w2, edge_vec, node_w1, node_b1, node_w2, node_vec):
        layers = edge_w1.shape[0]
        cols = node_lat.shape[2]
        nodes, edges = node_lat.shape[1], edge_lat.shape[1]
        npad = -(-nodes // TN) * TN
        eh = -(-edges // (2 * EC)) * EC
        nch = eh // EC
        dpn = mesh.shape['dp']
        per = SLABS // dpn
        dims = (layers, cols, nodes, edges, npad, eh, dpn)
        flat = lambda arr: jnp.swapaxes(arr, 1, 2)
        lead = lambda arr: jnp.transpose(arr, (1, 0, 2))
        args = (flat(node_lat), flat(edge_lat), flat(grad_node), flat(grad_edge), senders, receivers,
                edge_w1.reshape(-1, D), flat(edge_w2).reshape(-1, D), node_w1.reshape(-1, D), flat(node_w2).reshape(-1, D),
                lead(edge_vec), lead(node_vec), edge_b1, node_b1)
        vm, sem = pltpu.VMEM, pltpu.SemaphoreType.DMA
        wrows = -(-(HEAD + layers * LROWS) // (8 * dpn)) * 8 * dpn
        lat_n, lat_e = (2, cols, nodes), (2, cols, edges)
        outs = [RESULT(lat_n, BF), RESULT(lat_e, BF), RESULT(lat_n, BF), RESULT(lat_e, BF),
                RESULT((layers, 3, cols, D), F32), RESULT((layers, D), F32), RESULT((layers, cols, D), F32), RESULT((3, layers, cols), F32),
                RESULT((layers, 2, cols, D), F32), RESULT((layers, D), F32), RESULT((layers, cols, D), F32), RESULT((3, layers, cols), F32)]
        scratch = [
            *[vm(a.shape, a.dtype) for a in args[4:]], vm((wrows, D), F32), vm((3, wrows, D), F32),
            vm((2, cols, npad), F32), vm((3, cols, npad), F32), vm((2, cols, npad), F32), vm((3, cols, npad), F32),
            vm((cols, npad), F32), vm((cols, npad), F32), vm((cols, npad), F32), vm((cols, npad), F32),
            *[vm((3, nch, cols, EC), F32)] * 6,
            vm((2 * layers, D, npad), F32), vm((2 * layers, D, npad), F32),
            vm((layers, D, eh), F32), vm((layers, D, eh), F32), vm((8, eh), F32),
            vm((layers, D, npad), F32), vm((layers, D, npad), F32), vm((8, npad), F32),
            vm((D, npad), F32), vm((D, npad), F32), vm((D, npad), F32), vm((8, 2 * eh), jnp.int32), vm((D, D), F32), vm((layers, 2, 4 * D, D), F32),
            vm((layers, SLABS, D, D), F32), vm((layers, 2, SLABS, cols, D), F32), vm((layers, SLABS, 2, cols, D), F32),
            vm((layers, (dpn - 1) * per, 2, cols, D), F32), vm((layers, per, cols, D), F32), vm((layers, per, cols, D), F32),
            vm((layers, per, cols, D), F32), vm((layers, SLABS, cols, D), F32),
            sem((layers, 2)), sem((layers, 2)), sem((3, layers)), sem((3, layers)), sem((layers,)), sem((layers,)),
            sem((len(args),)), sem((3,)), sem((3,)), sem((3, 3)), sem((3, 3)), sem((4, 4)), sem((2, nch)), sem((2, 5)),
            sem((2 * layers,)), sem((2 * layers,)), pltpu.SemaphoreType.REGULAR]
        res = pl.pallas_call(
            lambda *refs: step_kernel(dims, *refs),
            name='graph_step',
            out_shape=outs,
            in_specs=[HB] * len(args),
            out_specs=[VM] * len(outs),
            scratch_shapes=scratch,
            compiler_params=pltpu.CompilerParams(collective_id=0, has_side_effects=True, vmem_limit_bytes=VMEM_LIMIT),
        )(*args)

        res = finish(res)
        return (flat(res[0]), flat(res[1]), flat(res[2]), flat(res[3]),
                res[4], res[5], flat(res[6]), lead(res[7]), res[8], res[9], flat(res[10]), lead(res[11]))

    return jax.shard_map(local_step, mesh=mesh, in_specs=in_specs, out_specs=out_specs, check_vma=False)
```

profile of v0, /device:TPU:0, one launch (start us, length us, event | category | flops | bytes accessed | tf_op | source)
XLA Modules:
  0.0 152.2 jit_solution(9291862178772172644)
XLA Ops:
  0.6 149.3 %graph_step.1 = (bf16[2,32,1885]{2,1,0:T(8,128)(2,1)S(1)}, bf16[2,32,10910]{2,1,0:T(8,128)(2,1)S(1)}, bf16[2,32,1885]{2,1,0:T(8,128)(2,1)S(1)}, bf16[2,32,10910]...) custom-call(bf16[2,32,1885]{2,1,0:T(8,128)(2,1)} %bitcast.24, ...), custom_call_target="tpu_custom_call" | custom-call | tf_op jit(solution)/shard_map/graph_step/pallas_call | solution.py:921
  149.9 2.2 %finish.1 = (bf16[2,32,1885]{2,1,0:T(8,128)(2,1)}, bf16[2,32,10910]{2,1,0:T(8,128)(2,1)}, bf16[2,32,1885]{2,1,0:T(8,128)(2,1)}, bf16[2,32,10910]{2,1,0:T(8,128)(...) custom-call(bf16[2,32,1885]{2,1,0:T(8,128)(2,1)S(1)} %get-tuple-elem, ...), custom_call_target="tpu_custom_call" | custom-call | tf_op jit(solution)/shard_map/finish/pallas_call | solution.py:865
where the time goes:
time: 152 us
  Pallas kernels  151 us (99%)
    pallas_call x1, Pallas kernels, local_step(): pl.pallas_call(lambda *refs: step_kernel(dims, *refs), name='graph_step',...  149 us

commit v1 on v0

--- a/solution.py
+++ b/solution.py
@@ -27,7 +27,6 @@
 LROWS = 7 * (D // 4)
 HEAD = 16
 LEADER = GROUP - 1
-FINISH_SEMS = 40
 VMEM_LIMIT = 63_000_000
 SLABS = 8
 EARLY = 6
@@ -168,7 +167,7 @@
     (send_ids, recv_ids, ew1_in, ew2_in, nw1_in, nw2_in, evec_in, nvec_in, eb1_in, nb1_in, w_send, w_recv, n_send, n_recv, gn_send, gn_recv, no_send, no_recv, dn_send, dn_recv,
      e_send, g_send, e_recv, g_recv, eo_recv, de_recv, part, part_recv, hidden, normed, inv, nhid, nnrm, ninv, d_part, s_sum, r_sum,
      ids_raw, bias_cols, sums, grad, core_recv, half, dp_recv, cross_send, cross_recv, own_sum, gathered,
-     core_ss, core_rs, dp_ss, dp_rs, cross_ss, cross_rs, load_sem, w_ss, w_rs, n_ss, n_rs, e_ss, e_rs, o_rs, p_ss, p_rs, ready) = refs[n_in + n_out:]
+     core_rs, dp_rs, cross_rs, w_rs, n_rs, e_rs, o_rs, p_rs, ready, load_sem, w_ss, n_ss, e_ss, p_ss, core_ss, dp_ss, cross_ss) = refs[n_in + n_out:]
 
     t = lax.axis_index('tp')
     p = lax.axis_index('dp')
@@ -850,7 +849,7 @@
 def finish_kernel(*refs):
     count = len(refs) // 2
     moves = sum((finish_moves(refs[k], refs[count + k]) for k in range(count)), [])
-    puts = [pltpu.make_async_copy(src, dst, refs[-1].at[k]) for k, (src, dst) in enumerate(moves)]
+    puts = [pltpu.make_async_copy(src, dst, refs[-1]) for src, dst in moves]
     for put in puts:
         put.start()
     for put in puts:
@@ -868,7 +867,7 @@
         out_shape=[jax.ShapeDtypeStruct(a.shape, a.dtype) for a in arrays],
         in_specs=[VM] * len(arrays),
         out_specs=[HB] * len(arrays),
-        scratch_shapes=[pltpu.SemaphoreType.DMA((FINISH_SEMS,))],
+        scratch_shapes=[pltpu.SemaphoreType.DMA],
         compiler_params=pltpu.CompilerParams(vmem_limit_bytes=1 << 20),
     )(*[keep_in_vmem(a) for a in arrays])
 
@@ -915,11 +914,11 @@
             vm((layers, SLABS, D, D), F32), vm((layers, 2, SLABS, cols, D), F32), vm((layers, SLABS, 2, cols, D), F32),
             vm((layers, (dpn - 1) * per, 2, cols, D), F32), vm((layers, per, cols, D), F32), vm((layers, per, cols, D), F32),
             vm((layers, per, cols, D), F32), vm((layers, SLABS, cols, D), F32),
-            sem((layers, 2)), sem((layers, 2)), sem((3, layers)), sem((3, layers)), sem((layers,)), sem((layers,)),
-            sem((len(args),)), sem((3,)), sem((3,)), sem((3, 3)), sem((3, 3)), sem((4, 4)), sem((2, nch)), sem((2, 5)),
-            sem((2 * layers,)), sem((2 * layers,)), pltpu.SemaphoreType.REGULAR]
+            sem((layers, 2)), sem((3, layers)), sem((layers,)), sem((3,)), sem((3, 3)), sem((2, nch)), sem((2, 5)), sem((2 * layers,)),
+            pltpu.SemaphoreType.REGULAR]
+        own_sems = [sem((len(args),)), sem((3,)), sem((3, 3)), sem((4, 4)), sem((2 * layers,)), sem((layers, 2)), sem((3, layers)), sem((layers,))]
         res = pl.pallas_call(
-            lambda *refs: step_kernel(dims, *refs),
+            lambda *refs: pl.run_scoped(lambda *own: step_kernel(dims, *refs, *own), *own_sems),
             name='graph_step',
             out_shape=outs,
             in_specs=[HB] * len(args),

time: 152 us -> 152 us (level)
  no operation moved by 1% of the time
where the time goes in v1:
time: 152 us; the launch traced here: 151 us
  Pallas kernels  151 us (99%)
    pallas_call x1, Pallas kernels, local_step(): pl.pallas_call(lambda *refs: pl.run_scoped(lambda *own: step_kernel(dims,...  149 us

profile of v1, /device:TPU:0, one launch (start us, length us, event | category | flops | bytes accessed | tf_op | source)
XLA Modules:
  0.0 151.4 jit_solution(6403986592220440418)
XLA Ops:
  0.6 148.8 %graph_step.1 = (bf16[2,32,1885]{2,1,0:T(8,128)(2,1)S(1)}, bf16[2,32,10910]{2,1,0:T(8,128)(2,1)S(1)}, bf16[2,32,1885]{2,1,0:T(8,128)(2,1)S(1)}, bf16[2,32,10910]...) custom-call(bf16[2,32,1885]{2,1,0:T(8,128)(2,1)} %bitcast.24, ...), custom_call_target="tpu_custom_call" | custom-call | tf_op jit(solution)/shard_map/graph_step/pallas_call | solution.py:920
  149.4 1.8 %finish.1 = (bf16[2,32,1885]{2,1,0:T(8,128)(2,1)}, bf16[2,32,10910]{2,1,0:T(8,128)(2,1)}, bf16[2,32,1885]{2,1,0:T(8,128)(2,1)}, bf16[2,32,10910]{2,1,0:T(8,128)(...) custom-call(bf16[2,32,1885]{2,1,0:T(8,128)(2,1)S(1)} %get-tuple-elem, ...), custom_call_target="tpu_custom_call" | custom-call | tf_op jit(solution)/shard_map/finish/pallas_call | solution.py:864

commit v2 on v1

--- a/solution.py
+++ b/solution.py
@@ -913,10 +913,11 @@
             vm((D, npad), F32), vm((D, npad), F32), vm((D, npad), F32), vm((8, 2 * eh), jnp.int32), vm((D, D), F32), vm((layers, 2, 4 * D, D), F32),
             vm((layers, SLABS, D, D), F32), vm((layers, 2, SLABS, cols, D), F32), vm((layers, SLABS, 2, cols, D), F32),
             vm((layers, (dpn - 1) * per, 2, cols, D), F32), vm((layers, per, cols, D), F32), vm((layers, per, cols, D), F32),
-            vm((layers, per, cols, D), F32), vm((layers, SLABS, cols, D), F32),
+            vm((layers, per, cols, D), F32), vm((layers, SLABS, cols, D), F32),]
+        own_sems = [
             sem((layers, 2)), sem((3, layers)), sem((layers,)), sem((3,)), sem((3, 3)), sem((2, nch)), sem((2, 5)), sem((2 * layers,)),
-            pltpu.SemaphoreType.REGULAR]
-        own_sems = [sem((len(args),)), sem((3,)), sem((3, 3)), sem((4, 4)), sem((2 * layers,)), sem((layers, 2)), sem((3, layers)), sem((layers,))]
+            pltpu.SemaphoreType.REGULAR,
+            sem((len(args),)), sem((3,)), sem((3, 3)), sem((4, 4)), sem((2 * layers,)), sem((layers, 2)), sem((3, layers)), sem((layers,))]
         res = pl.pallas_call(
             lambda *refs: pl.run_scoped(lambda *own: step_kernel(dims, *refs, *own), *own_sems),
             name='graph_step',

time: 152 us -> 151 us (level)
  no operation moved by 1% of the time
where the time goes in v2:
time: 151 us
  Pallas kernels  150 us (99%)
    pallas_call x1, Pallas kernels, local_step(): pl.pallas_call(lambda *refs: pl.run_scoped(lambda *own: step_kernel(dims,...  148 us

profile of v2, /device:TPU:0, one launch (start us, length us, event | category | flops | bytes accessed | tf_op | source)
XLA Modules:
  0.0 150.8 jit_solution(3783677776705543011)
XLA Ops:
  0.6 148.2 %graph_step.1 = (bf16[2,32,1885]{2,1,0:T(8,128)(2,1)S(1)}, bf16[2,32,10910]{2,1,0:T(8,128)(2,1)S(1)}, bf16[2,32,1885]{2,1,0:T(8,128)(2,1)S(1)}, bf16[2,32,10910]...) custom-call(bf16[2,32,1885]{2,1,0:T(8,128)(2,1)} %bitcast.24, ...), custom_call_target="tpu_custom_call" | custom-call | tf_op jit(solution)/shard_map/graph_step/pallas_call | solution.py:921
  148.9 1.8 %finish.1 = (bf16[2,32,1885]{2,1,0:T(8,128)(2,1)}, bf16[2,32,10910]{2,1,0:T(8,128)(2,1)}, bf16[2,32,1885]{2,1,0:T(8,128)(2,1)}, bf16[2,32,10910]{2,1,0:T(8,128)(...) custom-call(bf16[2,32,1885]{2,1,0:T(8,128)(2,1)S(1)} %get-tuple-elem, ...), custom_call_target="tpu_custom_call" | custom-call | tf_op jit(solution)/shard_map/finish/pallas_call | solution.py:864

commit v3 on v2

--- a/solution.py
+++ b/solution.py
@@ -165,7 +165,7 @@
     n_out = 12
     (node_raw, edge_raw, gnode_raw, gedge_raw, ew1_buf, eb1_buf, ew2_buf, evec_buf, nw1_buf, nb1_buf, nw2_buf, nvec_buf) = refs[n_in:n_in + n_out]
     (send_ids, recv_ids, ew1_in, ew2_in, nw1_in, nw2_in, evec_in, nvec_in, eb1_in, nb1_in, w_send, w_recv, n_send, n_recv, gn_send, gn_recv, no_send, no_recv, dn_send, dn_recv,
-     e_send, g_send, e_recv, g_recv, eo_recv, de_recv, part, part_recv, hidden, normed, inv, nhid, nnrm, ninv, d_part, s_sum, r_sum,
+     t_send, t_recv, e_send, g_send, e_recv, g_recv, eo_recv, de_recv, part, part_recv, hidden, normed, inv, nhid, nnrm, ninv, d_part, s_sum, r_sum,
      ids_raw, bias_cols, sums, grad, core_recv, half, dp_recv, cross_send, cross_recv, own_sum, gathered,
      core_rs, dp_rs, cross_rs, w_rs, n_rs, e_rs, o_rs, p_rs, ready, load_sem, w_ss, n_ss, e_ss, p_ss, core_ss, dp_ss, cross_ss) = refs[n_in + n_out:]
 
@@ -213,21 +213,41 @@
     def outward(kind):
         return kind in (EDGE_OUT, GRAD_OUT)
 
-    def edge_part(kind, index, send_sem, recv_sem, d):
+    every = slice(None)
+    ragged = pl.ds(D, D // GROUP)
+    rest = [slice(g * cols // GROUP, (g + 1) * cols // GROUP) for g in range(GROUP)]
+
+    def edge_part(kind, which, j, tail, send_sem, recv_sem, d):
         src, dst = buffers[kind]
+        if tail:
+            src, dst = t_send.at[kind % 2, which], t_recv.at[kind, which]
+        else:
+            src, dst = src.at[which, j], dst.at[which, j]
         recv_sems = o_rs.at[kind - EDGE_OUT, recv_sem] if outward(kind) else e_rs.at[kind, recv_sem]
-        return remote(src.at[index], dst.at[index], e_ss.at[kind, send_sem], recv_sems, d)
+        return remote(src, dst, e_ss.at[kind, send_sem], recv_sems, d)
 
     def by_half(half_id, j, action):
         narrow = jnp.logical_and(j == last, half_id == 1)
 
         @pl.when(jnp.logical_not(narrow))
         def _():
-            action(slice(None))
+            action(False)
 
         @pl.when(narrow)
         def _():
-            action(slice(T))
+            action(True)
+
+    def pack_tail(kind, d):
+        src, out = buffers[kind][0].at[slot(d), last], t_send.at[kind % 2, slot(d)]
+        out[:cols, :] = src[:, :D]
+        over = src[:, ragged]
+        out[cols:, :] = beside([over[r] for r in rest])
+
+    def unpack_tail(kind, d):
+        src, out = t_recv.at[kind, slot(d)], buffers[kind][1].at[slot(d), last]
+        out[:, :D] = src[:cols, :]
+        over = src[cols:, :]
+        out[:, ragged] = stacked([over[:, rows_of(g)] for g in range(GROUP)])
 
     def edge_start(kind, j, d):
         other = oc if d % 2 else c
@@ -235,29 +255,42 @@
             send_sem, recv_sem = jnp.where(j == last, 1, 0), jnp.where(j == last, 2 + slot(d), jnp.where(j < hold, 0, 1))
         else:
             send_sem, recv_sem = jnp.where(j == last, d, 0), j
-        by_half(c if outward(kind) else other, j,
-                lambda used: edge_part(kind, (slot(d), j, slice(None), used), send_sem, recv_sem, d).start())
+
+        def start(tail):
+            if tail:
+                pack_tail(kind, d)
+            edge_part(kind, slot(d), j, tail, send_sem, recv_sem, d).start()
+
+        by_half(c if outward(kind) else other, j, start)
 
     def edges_sent(kind):
-        every = slice(None)
-        edge_part(kind, (every, slice(0, last)), 0, 0, 1).wait_send()
+        edge_part(kind, every, slice(0, last), False, 0, 0, 1).wait_send()
         if outward(kind):
-            by_half(c, last, lambda used: edge_part(kind, (every, last, every, used), 1, 0, 1).wait_send())
+            by_half(c, last, lambda tail: edge_part(kind, every, last, tail, 1, 0, 1).wait_send())
         else:
             for d in OTHERS:
-                by_half(oc if d % 2 else c, last, lambda used: edge_part(kind, (slot(d), last, every, used), d, 0, d).wait_send())
+                by_half(oc if d % 2 else c, last, lambda tail: edge_part(kind, slot(d), last, tail, d, 0, d).wait_send())
 
     def chunk_arrived(kind, j):
-        every = slice(None)
-        by_half(c, j, lambda used: edge_part(kind, (every, j, every, used), 0, j, 1).wait_recv())
+        def arrived(tail):
+            edge_part(kind, every, j, tail, 0, j, 1).wait_recv()
+            if tail:
+                for d in OTHERS:
+                    unpack_tail(kind, d)
+
+        by_half(c, j, arrived)
 
     def group_arrived(kind, group):
-        every = slice(None)
         if group < 2:
-            edge_part(kind, (every, (slice(0, hold), slice(hold, last))[group]), 0, group, 1).wait_recv()
+            edge_part(kind, every, (slice(0, hold), slice(hold, last))[group], False, 0, group, 1).wait_recv()
         else:
             for d in OTHERS:
-                by_half(oc if d % 2 else c, last, lambda used: edge_part(kind, (slot(d), last, every, used), 0, 2 + slot(d), d).wait_recv())
+                def arrived(tail):
+                    edge_part(kind, slot(d), last, tail, 0, 2 + slot(d), d).wait_recv()
+                    if tail:
+                        unpack_tail(kind, d)
+
+                by_half(oc if d % 2 else c, last, arrived)
 
     def core_copy(l, b, stage):
         first, count = ((0, EARLY), (EARLY, SLABS - EARLY))[stage]
@@ -415,7 +448,7 @@
         @pl.when(c == 1)
         def _():
             for recv in (e_recv, g_recv):
-                recv[:, nch - 1, :, T:] = jnp.zeros((3, cols, EC - T), F32)
+                recv[:, last, :, D:] = jnp.zeros((len(OTHERS), cols, EC - D), F32)
 
         iota[...] = lax.broadcasted_iota(jnp.int32, (T, D), 0).astype(I16)
         lanes[...] = lax.broadcasted_iota(jnp.int32, (16, D), 1).astype(I16)
@@ -906,11 +939,11 @@
             *[vm(a.shape, a.dtype) for a in args[4:]], vm((wrows, D), F32), vm((3, wrows, D), F32),
             vm((2, cols, npad), F32), vm((3, cols, npad), F32), vm((2, cols, npad), F32), vm((3, cols, npad), F32),
             vm((cols, npad), F32), vm((cols, npad), F32), vm((cols, npad), F32), vm((cols, npad), F32),
-            *[vm((3, nch, cols, EC), F32)] * 6,
+            vm((2, 3, cols + cols // GROUP, D), F32), vm((4, 3, cols + cols // GROUP, D), F32), *[vm((3, nch, cols, EC), F32)] * 6,
             vm((2 * layers, D, npad), F32), vm((2 * layers, D, npad), F32),
-            vm((layers, D, eh), F32), vm((layers, D, eh), F32), vm((8, eh), F32),
-            vm((layers, D, npad), F32), vm((layers, D, npad), F32), vm((8, npad), F32),
-            vm((D, npad), F32), vm((D, npad), F32), vm((D, npad), F32), vm((8, 2 * eh), jnp.int32), vm((D, D), F32), vm((layers, 2, 4 * D, D), F32),
+            vm((layers, D, eh), F32), vm((layers, D, eh), F32), vm((layers, eh), F32),
+            vm((layers, D, npad), F32), vm((layers, D, npad), F32), vm((layers, npad), F32),
+            vm((D, npad), F32), vm((D, npad), F32), vm((D, npad), F32), vm((2, 2 * eh), jnp.int32), vm((D, D), F32), vm((layers, 2, 4 * D, D), F32),
             vm((layers, SLABS, D, D), F32), vm((layers, 2, SLABS, cols, D), F32), vm((layers, SLABS, 2, cols, D), F32),
             vm((layers, (dpn - 1) * per, 2, cols, D), F32), vm((layers, per, cols, D), F32), vm((layers, per, cols, D), F32),
             vm((layers, per, cols, D), F32), vm((layers, SLABS, cols, D), F32),]

time: 151 us -> 150 us (level)
  no operation moved by 1% of the time
where the time goes in v3:
time: 150 us
  Pallas kernels  149 us (99%)
    pallas_call x1, Pallas kernels, local_step(): pl.pallas_call(lambda *refs: pl.run_scoped(lambda *own: step_kernel(dims,...  147 us

profile of v3, /device:TPU:0, one launch (start us, length us, event | category | flops | bytes accessed | tf_op | source)
XLA Modules:
  0.0 149.9 jit_solution(3140159917478266773)
XLA Ops:
  0.6 147.2 %graph_step.1 = (bf16[2,32,1885]{2,1,0:T(8,128)(2,1)S(1)}, bf16[2,32,10910]{2,1,0:T(8,128)(2,1)S(1)}, bf16[2,32,1885]{2,1,0:T(8,128)(2,1)S(1)}, bf16[2,32,10910]...) custom-call(bf16[2,32,1885]{2,1,0:T(8,128)(2,1)} %bitcast.24, ...), custom_call_target="tpu_custom_call" | custom-call | tf_op jit(solution)/shard_map/graph_step/pallas_call | solution.py:954
  147.9 1.8 %finish.1 = (bf16[2,32,1885]{2,1,0:T(8,128)(2,1)}, bf16[2,32,10910]{2,1,0:T(8,128)(2,1)}, bf16[2,32,1885]{2,1,0:T(8,128)(2,1)}, bf16[2,32,10910]{2,1,0:T(8,128)(...) custom-call(bf16[2,32,1885]{2,1,0:T(8,128)(2,1)S(1)} %get-tuple-elem, ...), custom_call_target="tpu_custom_call" | custom-call | tf_op jit(solution)/shard_map/finish/pallas_call | solution.py:897

commit v4 on v3

--- a/solution.py
+++ b/solution.py
@@ -30,6 +30,7 @@
 VMEM_LIMIT = 63_000_000
 SLABS = 8
 EARLY = 6
+PAIR = 2
 VEC_SLAB = 5
 EDGE_SLABS = (0, 1, 6, 7)
 STAGES = (slice(0, EARLY), slice(EARLY, SLABS))
@@ -254,7 +255,7 @@
         if outward(kind):
             send_sem, recv_sem = jnp.where(j == last, 1, 0), jnp.where(j == last, 2 + slot(d), jnp.where(j < hold, 0, 1))
         else:
-            send_sem, recv_sem = jnp.where(j == last, d, 0), j
+            send_sem, recv_sem = d, last // PAIR
 
         def start(tail):
             if tail:
@@ -272,13 +273,19 @@
                 by_half(oc if d % 2 else c, last, lambda tail: edge_part(kind, slot(d), last, tail, d, 0, d).wait_send())
 
     def chunk_arrived(kind, j):
+        @pl.when(jnp.logical_and(lax.rem(j, PAIR) == 0, j < last))
+        def _():
+            edge_part(kind, every, pl.ds(j, PAIR), False, 0, j // PAIR, 1).wait_recv()
+
         def arrived(tail):
-            edge_part(kind, every, j, tail, 0, j, 1).wait_recv()
+            edge_part(kind, every, last, tail, 0, last // PAIR, 1).wait_recv()
             if tail:
                 for d in OTHERS:
                     unpack_tail(kind, d)
 
-        by_half(c, j, arrived)
+        @pl.when(j == last)
+        def _():
+            by_half(c, last, arrived)
 
     def group_arrived(kind, group):
         if group < 2:
@@ -342,12 +349,13 @@
                 send[slot(d), j] = val_of(sample, oc if d % 2 else c).astype(F32)
             own[:cols, lanes_j] = val_of(x, c)
 
-        def chunk(j):
-            put(j, at(j, EC), lambda s, h: raw[s, :, pl.ds(pl.multiple_of(h * eh + j * EC, D), EC)])
+        def pair(g):
+            for j in (PAIR * g, PAIR * g + 1):
+                put(j, at(j, EC), lambda s, h: raw[s, :, pl.ds(pl.multiple_of(h * eh + j * EC, D), EC)])
             for d in SEND_ORDER:
-                edge_start(kind, j, d)
-
-        loop(nch - 1, chunk)
+                edge_part(kind, slot(d), pl.ds(PAIR * g, PAIR), False, 0, g, d).start()
+
+        loop((nch - 1) // PAIR, pair)
         first = (nch - 1) * EC
         used = edges - eh - first
         last = pl.ds(first, EC)
@@ -948,7 +956,7 @@
             vm((layers, (dpn - 1) * per, 2, cols, D), F32), vm((layers, per, cols, D), F32), vm((layers, per, cols, D), F32),
             vm((layers, per, cols, D), F32), vm((layers, SLABS, cols, D), F32),]
         own_sems = [
-            sem((layers, 2)), sem((3, layers)), sem((layers,)), sem((3,)), sem((3, 3)), sem((2, nch)), sem((2, 5)), sem((2 * layers,)),
+            sem((layers, 2)), sem((3, layers)), sem((layers,)), sem((3,)), sem((3, 3)), sem((2, nch // PAIR + 1)), sem((2, 5)), sem((2 * layers,)),
             pltpu.SemaphoreType.REGULAR,
             sem((len(args),)), sem((3,)), sem((3, 3)), sem((4, 4)), sem((2 * layers,)), sem((layers, 2)), sem((3, layers)), sem((layers,))]
         res = pl.pallas_call(

time: 150 us -> 150 us (level)
  no operation moved by 1% of the time
where the time goes in v4:
time: 150 us
  Pallas kernels  149 us (99%)
    pallas_call x1, Pallas kernels, local_step(): pl.pallas_call(lambda *refs: pl.run_scoped(lambda *own: step_kernel(dims,...  147 us

profile of v4, /device:TPU:0, one launch (start us, length us, event | category | flops | bytes accessed | tf_op | source)
XLA Modules:
  0.0 149.9 jit_solution(12781370664655945815)
XLA Ops:
  0.6 147.2 %graph_step.1 = (bf16[2,32,1885]{2,1,0:T(8,128)(2,1)S(1)}, bf16[2,32,10910]{2,1,0:T(8,128)(2,1)S(1)}, bf16[2,32,1885]{2,1,0:T(8,128)(2,1)S(1)}, bf16[2,32,10910]...) custom-call(bf16[2,32,1885]{2,1,0:T(8,128)(2,1)} %bitcast.24, ...), custom_call_target="tpu_custom_call" | custom-call | tf_op jit(solution)/shard_map/graph_step/pallas_call | solution.py:962
  147.9 1.8 %finish.1 = (bf16[2,32,1885]{2,1,0:T(8,128)(2,1)}, bf16[2,32,10910]{2,1,0:T(8,128)(2,1)}, bf16[2,32,1885]{2,1,0:T(8,128)(2,1)}, bf16[2,32,10910]{2,1,0:T(8,128)(...) custom-call(bf16[2,32,1885]{2,1,0:T(8,128)(2,1)S(1)} %get-tuple-elem, ...), custom_call_target="tpu_custom_call" | custom-call | tf_op jit(solution)/shard_map/finish/pallas_call | solution.py:905

commit v5 on v3

--- a/solution.py
+++ b/solution.py
@@ -26,7 +26,7 @@
 SEND_ORDER = (2, 3, 1)
 LROWS = 7 * (D // 4)
 HEAD = 16
-LEADER = GROUP - 1
+LEADER = 0
 VMEM_LIMIT = 63_000_000
 SLABS = 8
 EARLY = 6

time: 150 us -> 151 us (level)
  no operation moved by 1% of the time
where the time goes in v5:
time: 151 us
  Pallas kernels  150 us (99%)
    pallas_call x1, Pallas kernels, local_step(): pl.pallas_call(lambda *refs: pl.run_scoped(lambda *own: step_kernel(dims,...  148 us

profile of v5, /device:TPU:0, one launch (start us, length us, event | category | flops | bytes accessed | tf_op | source)
XLA Modules:
  0.0 150.7 jit_solution(4897524534467782134)
XLA Ops:
  0.6 148.0 %graph_step.1 = (bf16[2,32,1885]{2,1,0:T(8,128)(2,1)S(1)}, bf16[2,32,10910]{2,1,0:T(8,128)(2,1)S(1)}, bf16[2,32,1885]{2,1,0:T(8,128)(2,1)S(1)}, bf16[2,32,10910]...) custom-call(bf16[2,32,1885]{2,1,0:T(8,128)(2,1)} %bitcast.24, ...), custom_call_target="tpu_custom_call" | custom-call | tf_op jit(solution)/shard_map/graph_step/pallas_call | solution.py:954
  148.7 1.8 %finish.1 = (bf16[2,32,1885]{2,1,0:T(8,128)(2,1)}, bf16[2,32,10910]{2,1,0:T(8,128)(2,1)}, bf16[2,32,1885]{2,1,0:T(8,128)(2,1)}, bf16[2,32,10910]{2,1,0:T(8,128)(...) custom-call(bf16[2,32,1885]{2,1,0:T(8,128)(2,1)S(1)} %get-tuple-elem, ...), custom_call_target="tpu_custom_call" | custom-call | tf_op jit(solution)/shard_map/finish/pallas_call | solution.py:897

commit v6 on v3

--- a/solution.py
+++ b/solution.py
@@ -27,6 +27,7 @@
 LROWS = 7 * (D // 4)
 HEAD = 16
 LEADER = GROUP - 1
+HELPER = LEADER - 1
 VMEM_LIMIT = 63_000_000
 SLABS = 8
 EARLY = 6
@@ -406,13 +407,14 @@
             @pl.when(t != LEADER)
             def _():
                 pl.semaphore_wait(barrier, len(OTHERS))
+
+            @pl.when(t == HELPER)
+            def _():
                 pl.semaphore_signal(ready, inc=1, device_id={'tp': LEADER}, device_id_type=MESH)
 
             @pl.when(t == LEADER)
             def _():
-                pl.semaphore_wait(ready, len(OTHERS))
-                for i in dp_others:
-                    pl.semaphore_signal(barrier, inc=1, device_id={'dp': lax.rem(p + i, dpn)}, device_id_type=MESH)
+                pl.semaphore_wait(ready, 1)
 
         w_cross.start()
         w_pair.start()
@@ -433,6 +435,8 @@
         with jax.named_scope('dp_barrier'):
             @pl.when(t == LEADER)
             def _():
+                for i in dp_others:
+                    pl.semaphore_signal(barrier, inc=1, device_id={'dp': lax.rem(p + i, dpn)}, device_id_type=MESH)
                 pl.semaphore_wait(barrier, len(OTHERS) + dpn - 1)
                 for d in OTHERS:
                     pl.semaphore_signal(ready, inc=1, device_id={'tp': peer[d]}, device_id_type=MESH)

time: 150 us -> 150 us (level)
  no operation moved by 1% of the time
where the time goes in v6:
time: 150 us
  Pallas kernels  149 us (99%)
    pallas_call x1, Pallas kernels, local_step(): pl.pallas_call(lambda *refs: pl.run_scoped(lambda *own: step_kernel(dims,...  147 us

profile of v6, /device:TPU:0, one launch (start us, length us, event | category | flops | bytes accessed | tf_op | source)
XLA Modules:
  0.0 149.7 jit_solution(9046380228038747940)
XLA Ops:
  0.6 147.0 %graph_step.1 = (bf16[2,32,1885]{2,1,0:T(8,128)(2,1)S(1)}, bf16[2,32,10910]{2,1,0:T(8,128)(2,1)S(1)}, bf16[2,32,1885]{2,1,0:T(8,128)(2,1)S(1)}, bf16[2,32,10910]...) custom-call(bf16[2,32,1885]{2,1,0:T(8,128)(2,1)} %bitcast.24, ...), custom_call_target="tpu_custom_call" | custom-call | tf_op jit(solution)/shard_map/graph_step/pallas_call | solution.py:958
  147.7 1.8 %finish.1 = (bf16[2,32,1885]{2,1,0:T(8,128)(2,1)}, bf16[2,32,10910]{2,1,0:T(8,128)(2,1)}, bf16[2,32,1885]{2,1,0:T(8,128)(2,1)}, bf16[2,32,10910]{2,1,0:T(8,128)(...) custom-call(bf16[2,32,1885]{2,1,0:T(8,128)(2,1)S(1)} %get-tuple-elem, ...), custom_call_target="tpu_custom_call" | custom-call | tf_op jit(solution)/shard_map/finish/pallas_call | solution.py:901

commit v7 on v6

--- a/solution.py
+++ b/solution.py
@@ -166,7 +166,7 @@
     n_out = 12
     (node_raw, edge_raw, gnode_raw, gedge_raw, ew1_buf, eb1_buf, ew2_buf, evec_buf, nw1_buf, nb1_buf, nw2_buf, nvec_buf) = refs[n_in:n_in + n_out]
     (send_ids, recv_ids, ew1_in, ew2_in, nw1_in, nw2_in, evec_in, nvec_in, eb1_in, nb1_in, w_send, w_recv, n_send, n_recv, gn_send, gn_recv, no_send, no_recv, dn_send, dn_recv,
-     t_send, t_recv, e_send, g_send, e_recv, g_recv, eo_recv, de_recv, part, part_recv, hidden, normed, inv, nhid, nnrm, ninv, d_part, s_sum, r_sum,
+     node_pad, t_send, t_recv, e_send, g_send, e_recv, g_recv, eo_recv, de_recv, part, part_recv, hidden, normed, inv, nhid, nnrm, ninv, d_part, s_sum, r_sum,
      ids_raw, bias_cols, sums, grad, core_recv, half, dp_recv, cross_send, cross_recv, own_sum, gathered,
      core_rs, dp_rs, cross_rs, w_rs, n_rs, e_rs, o_rs, p_rs, ready, load_sem, w_ss, n_ss, e_ss, p_ss, core_ss, dp_ss, cross_ss) = refs[n_in + n_out:]
 
@@ -327,14 +327,56 @@
     def gather_copy(l, i, owner):
         return dp_remote(own_sum.at[l], gathered.at[l, pl.ds(seat(owner) * per, per)], 1, l, i)
 
+    def part_piece(q, a):
+        return remote(part.at[q, :, a], part_recv.at[q, :, a], p_ss.at[q], p_rs.at[q], 1)
+
     def part_copy(q):
         return remote(part.at[q], part_recv.at[q], p_ss.at[q], p_rs.at[q], 1)
 
+    wide = D // GROUP
+    tiles = nodes // D
+    over = range(tiles * D, nodes, wide)
+
+    def node_rows(k):
+        return slice(k * cols, (k + 1) * cols) if k < tiles else pl.ds(tiles * cols + (k - tiles) * cols // GROUP, cols // GROUP)
+
+    def pack_nodes(take, out):
+        for k in range(tiles):
+            out[node_rows(k), :] = take(k * D, D)
+        for k, start in enumerate(over):
+            val = take(start, wide)
+            out[node_rows(tiles + k), :] = beside([val[r] for r in rest])
+
+    def unpack_nodes(src, put):
+        for k in range(tiles):
+            put(k * D, src[node_rows(k), :])
+        for k, start in enumerate(over):
+            val = src[node_rows(tiles + k), :]
+            put(start, stacked([val[:, rows_of(g)] for g in range(GROUP)]))
+
+    def put_rows(ref, rows):
+        def put(start, val):
+            ref[rows, start:start + val.shape[1]] = val.astype(ref.dtype)
+
+        return put
+
+    def put_output(ref):
+        def put(start, val):
+            used = min(val.shape[1], nodes - start)
+            ref[ox, :, start:start + used] = val[:, :used].astype(ref.dtype)
+
+        return put
+
+    def take_rows(ref, rows):
+        return lambda start, width: ref[rows, start:start + width].astype(F32)
+
     def load_nodes(raw, send, own):
-        send[...] = jnp.zeros_like(send)
-        send[0, :, :nodes] = raw[ox].astype(F32)
-        send[1, :, :nodes] = raw[x].astype(F32)
-        own[:cols, :] = send[1].astype(own.dtype)
+        own[...] = jnp.zeros_like(own)
+        node_pad[...] = jnp.zeros_like(node_pad)
+        for which, sample in enumerate((ox, x)):
+            node_pad[:, :nodes] = raw[sample].astype(F32)
+            pack_nodes(take_rows(node_pad, every), send.at[which])
+        own[:cols, :] = node_pad[...].astype(own.dtype)
 
     def load_edges(raw, send, own, kind):
         def put(j, lanes_j, val_of):
@@ -384,7 +426,7 @@
 
         barrier = pltpu.get_barrier_semaphore()
         for d in OTHERS:
-            pl.semaphore_signal(barrier, inc=1, device_id={'tp': peer[d]}, device_id_type=MESH)
+            pl.semaphore_signal(barrier, device_id={'tp': peer[d]}, device_id_type=MESH)
         for copy in loads[:1] + loads[4:] + loads[1:4]:
             copy.start()
         loads[0].wait()
@@ -410,7 +452,7 @@
 
             @pl.when(t == HELPER)
             def _():
-                pl.semaphore_signal(ready, inc=1, device_id={'tp': LEADER}, device_id_type=MESH)
+                pl.semaphore_signal(ready, device_id={'tp': LEADER}, device_id_type=MESH)
 
             @pl.when(t == LEADER)
             def _():
@@ -436,10 +478,10 @@
             @pl.when(t == LEADER)
             def _():
                 for i in dp_others:
-                    pl.semaphore_signal(barrier, inc=1, device_id={'dp': lax.rem(p + i, dpn)}, device_id_type=MESH)
+                    pl.semaphore_signal(barrier, device_id={'dp': lax.rem(p + i, dpn)}, device_id_type=MESH)
                 pl.semaphore_wait(barrier, len(OTHERS) + dpn - 1)
                 for d in OTHERS:
-                    pl.semaphore_signal(ready, inc=1, device_id={'tp': peer[d]}, device_id_type=MESH)
+                    pl.semaphore_signal(ready, device_id={'tp': peer[d]}, device_id_type=MESH)
 
             @pl.when(t != LEADER)
             def _():
@@ -505,7 +547,7 @@
         with jax.named_scope('node_wait'):
             wait_recvs(ncop)
         for d in OTHERS:
-            v0[rows_of(d), :] = n_recv[slot(d)].astype(BF)
+            unpack_nodes(n_recv.at[slot(d)], put_rows(v0, rows_of(d)))
         with jax.named_scope('weight_wait'):
             dp_all(0, 2).wait_recv()
             w_relay.start()
@@ -609,7 +651,7 @@
                 part_copy(l).wait_recv()
             with jax.named_scope(f'node_forward_{l}'):
                 node_forward(l)
-        no_send[...] = tables[layers][rows_of(2), :].astype(F32)
+        pack_nodes(take_rows(tables[layers], rows_of(2)), no_send)
         no_copy = remote(no_send, no_recv, n_ss.at[2, 0], n_rs.at[2, 0], 2)
         no_copy.start()
         node_raw[x] = tables[layers][:q, :nodes]
@@ -620,7 +662,7 @@
             gcop[0].wait_recv()
             gcop[2].wait_recv()
         for d in OTHERS:
-            d_part[rows_of(d), :] = gn_recv[slot(d)]
+            unpack_nodes(gn_recv.at[slot(d)], put_rows(d_part, rows_of(d)))
 
         def node_backward(l):
             table, agg = tables[l], aggs[l]
@@ -743,6 +785,8 @@
                 a = pl.ds(pl.multiple_of(step * TN, D), TN)
                 s_bf, r_bf, v_in = s_sum[:, a].astype(BF), r_sum[:, a].astype(BF), table[:, a]
                 part[layers + l, :, a] = dot(ew1[l, mat(1), :], s_bf) + dot(ew1[l, mat(2), :], r_bf)
+                if l > 0:
+                    part_piece(layers + l, a).start()
                 grad[l, 6] += dot_nt(v_in, s_bf)
                 grad[l, 7] += dot_nt(v_in, r_bf)
 
@@ -778,7 +822,8 @@
             with jax.named_scope(f'project_{l}'):
                 project(l)
             reduce_start(l, 1)
-            part_copy(layers + l).start()
+            if first_layer:
+                part_copy(layers + l).start()
             if first_layer:
                 with jax.named_scope('chip_sum_late'):
                     chip_sum(0, 1)
@@ -797,7 +842,7 @@
         with jax.named_scope('dp_sum_late'):
             dp_sum(0, 1)
 
-        dn_send[...] = v2[rows_of(2), :].astype(F32)
+        pack_nodes(take_rows(v2, rows_of(2)), dn_send)
         dn_copy = remote(dn_send, dn_recv, n_ss.at[2, 1], n_rs.at[2, 1], 2)
         dn_copy.start()
 
@@ -809,7 +854,7 @@
 
         with jax.named_scope('node_out_wait'):
             no_copy.wait_recv()
-        node_raw[ox] = no_recv[:, :nodes].astype(BF)
+        unpack_nodes(no_recv, put_output(node_raw))
 
         def place_e(j):
             for d in OTHERS:
@@ -832,7 +877,7 @@
                 cross_sum(l)
         with jax.named_scope('d_node_wait'):
             dn_copy.wait_recv()
-        gnode_raw[ox] = dn_recv[:, :nodes].astype(BF)
+        unpack_nodes(dn_recv, put_output(gnode_raw))
         with jax.named_scope('place_rest'):
             group_arrived(GRAD_OUT, 1)
             loop(last, place_g, hold)
@@ -934,6 +979,7 @@
                 edge_w1.reshape(-1, D), flat(edge_w2).reshape(-1, D), node_w1.reshape(-1, D), flat(node_w2).reshape(-1, D),
                 lead(edge_vec), lead(node_vec), edge_b1, node_b1)
         vm, sem = pltpu.VMEM, pltpu.SemaphoreType.DMA
+        packed = nodes // D * cols + -(-(nodes % D) * GROUP // D) * cols // GROUP
         wrows = -(-(HEAD + layers * LROWS) // (8 * dpn)) * 8 * dpn
         lat_n, lat_e = (2, cols, nodes), (2, cols, edges)
         outs = [RESULT(lat_n, BF), RESULT(lat_e, BF), RESULT(lat_n, BF), RESULT(lat_e, BF),
@@ -941,8 +987,7 @@
                 RESULT((layers, 2, cols, D), F32), RESULT((layers, D), F32), RESULT((layers, cols, D), F32), RESULT((3, layers, cols), F32)]
         scratch = [
             *[vm(a.shape, a.dtype) for a in args[4:]], vm((wrows, D), F32), vm((3, wrows, D), F32),
-            vm((2, cols, npad), F32), vm((3, cols, npad), F32), vm((2, cols, npad), F32), vm((3, cols, npad), F32),
-            vm((cols, npad), F32), vm((cols, npad), F32), vm((cols, npad), F32), vm((cols, npad), F32),
+            *[vm((many, packed, D), F32) for many in (2, 3, 2, 3)], *[vm((packed, D), F32)] * 4, vm((cols, npad), F32),
             vm((2, 3, cols + cols // GROUP, D), F32), vm((4, 3, cols + cols // GROUP, D), F32), *[vm((3, nch, cols, EC), F32)] * 6,
             vm((2 * layers, D, npad), F32), vm((2 * layers, D, npad), F32),
             vm((layers, D, eh), F32), vm((layers, D, eh), F32), vm((layers, eh), F32),

time: 150 us -> 150 us (level)
  no operation moved by 1% of the time
where the time goes in v7:
time: 150 us; the launch traced here: 149 us
  Pallas kernels  149 us (99%)
    pallas_call x1, Pallas kernels, local_step(): pl.pallas_call(lambda *refs: pl.run_scoped(lambda *own: step_kernel(dims,...  147 us

profile of v7, /device:TPU:0, one launch (start us, length us, event | category | flops | bytes accessed | tf_op | source)
XLA Modules:
  0.0 149.4 jit_solution(8344572454019332416)
XLA Ops:
  0.6 146.8 %graph_step.1 = (bf16[2,32,1885]{2,1,0:T(8,128)(2,1)S(1)}, bf16[2,32,10910]{2,1,0:T(8,128)(2,1)S(1)}, bf16[2,32,1885]{2,1,0:T(8,128)(2,1)S(1)}, bf16[2,32,10910]...) custom-call(bf16[2,32,1885]{2,1,0:T(8,128)(2,1)} %bitcast.24, ...), custom_call_target="tpu_custom_call" | custom-call | tf_op jit(solution)/shard_map/graph_step/pallas_call | solution.py:1003
  147.5 1.8 %finish.1 = (bf16[2,32,1885]{2,1,0:T(8,128)(2,1)}, bf16[2,32,10910]{2,1,0:T(8,128)(2,1)}, bf16[2,32,1885]{2,1,0:T(8,128)(2,1)}, bf16[2,32,10910]{2,1,0:T(8,128)(...) custom-call(bf16[2,32,1885]{2,1,0:T(8,128)(2,1)S(1)} %get-tuple-elem, ...), custom_call_target="tpu_custom_call" | custom-call | tf_op jit(solution)/shard_map/finish/pallas_call | solution.py:946

commit v8 on v7

--- a/solution.py
+++ b/solution.py
@@ -184,7 +184,8 @@
 
     small_in = (send_ids, recv_ids, ew1_in, ew2_in, nw1_in, nw2_in, evec_in, nvec_in, eb1_in, nb1_in)
     loads = [pltpu.make_async_copy(src, dst, load_sem.at[q]) for q, (src, dst) in enumerate(
-        zip(hbm_in, (node_raw, edge_raw, gnode_raw, gedge_raw) + small_in))]
+        zip((hbm_in[0].at[x],) + hbm_in[1:], (node_raw.at[x], edge_raw, gnode_raw, gedge_raw) + small_in))]
+    first_load = pltpu.make_async_copy(hbm_in[0].at[ox], node_raw.at[ox], load_sem.at[n_in])
 
     def node_copies(send, recv, kind):
         return (remote(send.at[1], recv.at[0], n_ss.at[kind, 0], n_rs.at[kind, 0], 1),
@@ -370,12 +371,12 @@
     def take_rows(ref, rows):
         return lambda start, width: ref[rows, start:start + width].astype(F32)
 
-    def load_nodes(raw, send, own):
+    def load_nodes(raw, sample, out):
+        node_pad[:, :nodes] = raw[sample].astype(F32)
+        pack_nodes(take_rows(node_pad, every), out)
+
+    def keep_nodes(own):
         own[...] = jnp.zeros_like(own)
-        node_pad[...] = jnp.zeros_like(node_pad)
-        for which, sample in enumerate((ox, x)):
-            node_pad[:, :nodes] = raw[sample].astype(F32)
-            pack_nodes(take_rows(node_pad, every), send.at[which])
         own[:cols, :] = node_pad[...].astype(own.dtype)
 
     def load_edges(raw, send, own, kind):
@@ -427,12 +428,31 @@
         barrier = pltpu.get_barrier_semaphore()
         for d in OTHERS:
             pl.semaphore_signal(barrier, device_id={'tp': peer[d]}, device_id_type=MESH)
-        for copy in loads[:1] + loads[4:] + loads[1:4]:
+        for copy in [first_load] + loads[:1] + loads[4:] + loads[1:4]:
             copy.start()
+        node_pad[...] = jnp.zeros_like(node_pad)
+        with jax.named_scope('barrier'):
+            @pl.when(t != LEADER)
+            def _():
+                pl.semaphore_wait(barrier, len(OTHERS))
+
+            @pl.when(t == HELPER)
+            def _():
+                pl.semaphore_signal(ready, device_id={'tp': LEADER}, device_id_type=MESH)
+
+            @pl.when(t == LEADER)
+            def _():
+                pl.semaphore_wait(ready, 1)
+
+        first_load.wait()
+        with jax.named_scope('send_nodes'):
+            load_nodes(node_raw, ox, n_send.at[0])
+        ncop = node_copies(n_send, n_recv, 0)
+        ncop[1].start()
         loads[0].wait()
-        with jax.named_scope('send_nodes'):
-            load_nodes(node_raw, n_send, v0)
-        ncop = node_copies(n_send, n_recv, 0)
+        load_nodes(node_raw, x, n_send.at[1])
+        keep_nodes(v0)
+        ncop[0].start()
         for copy in loads[4:]:
             copy.wait()
         q = cols
@@ -445,28 +465,15 @@
             w_send[packed(l, 3), :] = ew2_in[pl.ds(l * q, q), :].astype(F32)
             w_send[packed(l, 4, 2), :] = nw1_in[pl.ds(l * 2 * q, 2 * q), :].astype(F32)
             w_send[packed(l, 6), :] = nw2_in[pl.ds(l * q, q), :].astype(F32)
-        with jax.named_scope('barrier'):
-            @pl.when(t != LEADER)
-            def _():
-                pl.semaphore_wait(barrier, len(OTHERS))
-
-            @pl.when(t == HELPER)
-            def _():
-                pl.semaphore_signal(ready, device_id={'tp': LEADER}, device_id_type=MESH)
-
-            @pl.when(t == LEADER)
-            def _():
-                pl.semaphore_wait(ready, 1)
-
         w_cross.start()
         w_pair.start()
-        ncop[1].start()
-        ncop[0].start()
         loads[1].wait()
         with jax.named_scope('send_edges'):
             load_edges(edge_raw, e_send, e0, EDGE_IN)
         loads[2].wait()
-        load_nodes(gnode_raw, gn_send, d_part)
+        load_nodes(gnode_raw, ox, gn_send.at[0])
+        load_nodes(gnode_raw, x, gn_send.at[1])
+        keep_nodes(d_part)
         gcop = node_copies(gn_send, gn_recv, 1)
         gcop[1].start()
         gcop[0].start()
@@ -999,7 +1006,7 @@
         own_sems = [
             sem((layers, 2)), sem((3, layers)), sem((layers,)), sem((3,)), sem((3, 3)), sem((2, nch)), sem((2, 5)), sem((2 * layers,)),
             pltpu.SemaphoreType.REGULAR,
-            sem((len(args),)), sem((3,)), sem((3, 3)), sem((4, 4)), sem((2 * layers,)), sem((layers, 2)), sem((3, layers)), sem((layers,))]
+            sem((len(args) + 1,)), sem((3,)), sem((3, 3)), sem((4, 4)), sem((2 * layers,)), sem((layers, 2)), sem((3, layers)), sem((layers,))]
         res = pl.pallas_call(
             lambda *refs: pl.run_scoped(lambda *own: step_kernel(dims, *refs, *own), *own_sems),
             name='graph_step',

time: 150 us -> 149 us (level)
  no operation moved by 1% of the time
where the time goes in v8:
time: 149 us
  Pallas kernels  148 us (99%)
    pallas_call x1, Pallas kernels, local_step(): pl.pallas_call(lambda *refs: pl.run_scoped(lambda *own: step_kernel(dims,...  146 us

profile of v8, /device:TPU:0, one launch (start us, length us, event | category | flops | bytes accessed | tf_op | source)
XLA Modules:
  0.0 148.6 jit_solution(7252690498867106170)
XLA Ops:
  0.6 146.0 %graph_step.1 = (bf16[2,32,1885]{2,1,0:T(8,128)(2,1)S(1)}, bf16[2,32,10910]{2,1,0:T(8,128)(2,1)S(1)}, bf16[2,32,1885]{2,1,0:T(8,128)(2,1)S(1)}, bf16[2,32,10910]...) custom-call(bf16[2,32,1885]{2,1,0:T(8,128)(2,1)} %bitcast.24, ...), custom_call_target="tpu_custom_call" | custom-call | tf_op jit(solution)/shard_map/graph_step/pallas_call | solution.py:1010
  146.7 1.8 %finish.1 = (bf16[2,32,1885]{2,1,0:T(8,128)(2,1)}, bf16[2,32,10910]{2,1,0:T(8,128)(2,1)}, bf16[2,32,1885]{2,1,0:T(8,128)(2,1)}, bf16[2,32,10910]{2,1,0:T(8,128)(...) custom-call(bf16[2,32,1885]{2,1,0:T(8,128)(2,1)S(1)} %get-tuple-elem, ...), custom_call_target="tpu_custom_call" | custom-call | tf_op jit(solution)/shard_map/finish/pallas_call | solution.py:953

commit v9 on v8

--- a/solution.py
+++ b/solution.py
@@ -165,7 +165,7 @@
     hbm_in = refs[:n_in]
     n_out = 12
     (node_raw, edge_raw, gnode_raw, gedge_raw, ew1_buf, eb1_buf, ew2_buf, evec_buf, nw1_buf, nb1_buf, nw2_buf, nvec_buf) = refs[n_in:n_in + n_out]
-    (send_ids, recv_ids, ew1_in, ew2_in, nw1_in, nw2_in, evec_in, nvec_in, eb1_in, nb1_in, w_send, w_recv, n_send, n_recv, gn_send, gn_recv, no_send, no_recv, dn_send, dn_recv,
+    (send_ids, recv_ids, ew1_in, ew2_in, nw1_in, nw2_in, evec_in, nvec_in, eb1_in, nb1_in, w_send, w_recv, n_send, n_recv, gn_send, gn_recv, no_recv, dn_recv,
      node_pad, t_send, t_recv, e_send, g_send, e_recv, g_recv, eo_recv, de_recv, part, part_recv, hidden, normed, inv, nhid, nnrm, ninv, d_part, s_sum, r_sum,
      ids_raw, bias_cols, sums, grad, core_recv, half, dp_recv, cross_send, cross_recv, own_sum, gathered,
      core_rs, dp_rs, cross_rs, w_rs, n_rs, e_rs, o_rs, p_rs, ready, load_sem, w_ss, n_ss, e_ss, p_ss, core_ss, dp_ss, cross_ss) = refs[n_in + n_out:]
@@ -176,7 +176,8 @@
     dp_others = range(1, dpn)
     x, c = t // 2, lax.rem(t, 2)
     ox, oc = 1 - x, 1 - c
-    peer = [t, t + 1 - 2 * c, t + 2 - 4 * x, t + 3 - 2 * c - 4 * x]
+    mate, across = t + oc - c, t + 2 * (ox - x)
+    peer = [t, mate, across, mate + across - t]
 
     def remote(src, dst, ssem, rsem, d):
         return pltpu.make_async_remote_copy(src_ref=src, dst_ref=dst, send_sem=ssem, recv_sem=rsem,
@@ -185,6 +186,7 @@
     small_in = (send_ids, recv_ids, ew1_in, ew2_in, nw1_in, nw2_in, evec_in, nvec_in, eb1_in, nb1_in)
     loads = [pltpu.make_async_copy(src, dst, load_sem.at[q]) for q, (src, dst) in enumerate(
         zip((hbm_in[0].at[x],) + hbm_in[1:], (node_raw.at[x], edge_raw, gnode_raw, gedge_raw) + small_in))]
+    node_load, edge_load, gnode_load, gedge_load, *small_loads = loads
     first_load = pltpu.make_async_copy(hbm_in[0].at[ox], node_raw.at[ox], load_sem.at[n_in])
 
     def node_copies(send, recv, kind):
@@ -210,6 +212,8 @@
 
     last = nch - 1
     hold = nch - 3
+    share = 2 * (eh - last * EC - D - D // GROUP) * cols // D
+    share = min(share, no_recv.shape[0] // 16 * 8)
     buffers = ((e_send, e_recv), (g_send, g_recv), (e_send, eo_recv), (g_send, de_recv))
 
     def outward(kind):
@@ -295,12 +299,11 @@
                 by_half(oc if d % 2 else c, last, arrived)
 
     def core_copy(l, b, stage):
-        first, count = ((0, EARLY), (EARLY, SLABS - EARLY))[stage]
-        return remote(grad.at[l, pl.ds(first, count), pl.ds((2 * b + 1) * cols, cols), :], core_recv.at[l, b, pl.ds(first, count)],
+        return remote(grad.at[l, STAGES[stage], pl.ds((2 * b + 1) * cols, cols), :], core_recv.at[l, b, STAGES[stage]],
                       core_ss.at[l, stage], core_rs.at[l, stage], 1)
 
     def core_all(l, stage):
-        part_of = core_recv.at[l, :, (slice(0, EARLY), slice(EARLY, SLABS))[stage]]
+        part_of = core_recv.at[l, :, STAGES[stage]]
         return remote(part_of, part_of, core_ss.at[l, stage], core_rs.at[l, stage], 1)
 
     def seat(device):
@@ -319,7 +322,7 @@
 
     def dp_all(l, stage):
         most = (dpn - 1) * per
-        part_of = (dp_recv.at[l], gathered.at[l, pl.ds(0, most)], w_recv.at[1, pl.ds(0, (dpn - 1) * piece)])[stage]
+        part_of = (dp_recv.at[l], gathered.at[l, slice(most)], w_recv.at[1, slice((dpn - 1) * piece)])[stage]
         return dp_remote(part_of, part_of, stage, l, 1)
 
     def cross_copy(l):
@@ -327,6 +330,26 @@
 
     def gather_copy(l, i, owner):
         return dp_remote(own_sum.at[l], gathered.at[l, pl.ds(seat(owner) * per, per)], 1, l, i)
+
+    def output_copies(action):
+        block, more = n_send.at[0], n_send.at[1]
+        most = slice(block.shape[0] - share)
+        end = pl.ds(block.shape[0] - share, share)
+        sems = n_ss.at[2, 0], n_rs.at[2, 0]
+        extra = remote(more.at[end], no_recv.at[end], n_ss.at[2, 2], n_rs.at[2, 2], 3)
+        first_core = c == 0
+
+        @pl.when(first_core)
+        def _():
+            getattr(remote(block.at[most], no_recv.at[most], *sems, 2), action)()
+            if action == 'wait_recv':
+                extra.wait_recv()
+
+        @pl.when(jnp.logical_not(first_core))
+        def _():
+            getattr(remote(block, no_recv, *sems, 2), action)()
+            if action != 'wait_recv':
+                getattr(extra, action)()
 
     def part_piece(q, a):
         return remote(part.at[q, :, a], part_recv.at[q, :, a], p_ss.at[q], p_rs.at[q], 1)
@@ -428,7 +451,7 @@
         barrier = pltpu.get_barrier_semaphore()
         for d in OTHERS:
             pl.semaphore_signal(barrier, device_id={'tp': peer[d]}, device_id_type=MESH)
-        for copy in [first_load] + loads[:1] + loads[4:] + loads[1:4]:
+        for copy in (first_load, node_load, *small_loads, edge_load, gnode_load, gedge_load):
             copy.start()
         node_pad[...] = jnp.zeros_like(node_pad)
         with jax.named_scope('barrier'):
@@ -449,11 +472,11 @@
             load_nodes(node_raw, ox, n_send.at[0])
         ncop = node_copies(n_send, n_recv, 0)
         ncop[1].start()
-        loads[0].wait()
+        node_load.wait()
         load_nodes(node_raw, x, n_send.at[1])
         keep_nodes(v0)
         ncop[0].start()
-        for copy in loads[4:]:
+        for copy in small_loads:
             copy.wait()
         q = cols
         w_send[:HEAD, :] = jnp.zeros((HEAD, D), F32)
@@ -467,17 +490,17 @@
             w_send[packed(l, 6), :] = nw2_in[pl.ds(l * q, q), :].astype(F32)
         w_cross.start()
         w_pair.start()
-        loads[1].wait()
+        edge_load.wait()
         with jax.named_scope('send_edges'):
             load_edges(edge_raw, e_send, e0, EDGE_IN)
-        loads[2].wait()
+        gnode_load.wait()
         load_nodes(gnode_raw, ox, gn_send.at[0])
         load_nodes(gnode_raw, x, gn_send.at[1])
         keep_nodes(d_part)
         gcop = node_copies(gn_send, gn_recv, 1)
         gcop[1].start()
         gcop[0].start()
-        loads[3].wait()
+        gedge_load.wait()
         with jax.named_scope('send_grads'):
             load_edges(gedge_raw, g_send, ge, GRAD_IN)
 
@@ -658,9 +681,11 @@
                 part_copy(l).wait_recv()
             with jax.named_scope(f'node_forward_{l}'):
                 node_forward(l)
-        pack_nodes(take_rows(tables[layers], rows_of(2)), no_send)
-        no_copy = remote(no_send, no_recv, n_ss.at[2, 0], n_rs.at[2, 0], 2)
-        no_copy.start()
+        for copy in ncop[:2]:
+            copy.wait_send()
+        for which in BOTH:
+            pack_nodes(take_rows(tables[layers], rows_of(2 + which)), n_send.at[which])
+        output_copies('start')
         node_raw[x] = tables[layers][:q, :nodes]
 
         grad[...] = jnp.zeros_like(grad)
@@ -759,7 +784,9 @@
                     if k in EDGE_SLABS:
                         own = own + core_recv[l, b, k]
                     elif k == VEC_SLAB:
-                        own = own + jnp.where(edge_row, core_recv[l, b, k], 0.0)
+                        other = core_recv[l, b, k]
+                        own = own + jnp.where(edge_row, other, 0.0)
+                        own = jnp.where(jnp.logical_and(row == 7, c == 1), other, own)
                     half[l, k, b] = own
             for i in dp_others:
                 @pl.when(in_stage(lax.rem(p + i, dpn), stage))
@@ -849,6 +876,8 @@
         with jax.named_scope('dp_sum_late'):
             dp_sum(0, 1)
 
+        gcop[1].wait_send()
+        dn_send = gn_send.at[0]
         pack_nodes(take_rows(v2, rows_of(2)), dn_send)
         dn_copy = remote(dn_send, dn_recv, n_ss.at[2, 1], n_rs.at[2, 1], 2)
         dn_copy.start()
@@ -860,7 +889,7 @@
         loop(nch, send_rest, hold)
 
         with jax.named_scope('node_out_wait'):
-            no_copy.wait_recv()
+            output_copies('wait_recv')
         unpack_nodes(no_recv, put_output(node_raw))
 
         def place_e(j):
@@ -907,10 +936,10 @@
             cross_copy(l).wait_send()
             dp_all(l, 0).wait_send()
             dp_all(l, 1).wait_send()
-        for copy in ncop + gcop + (w_pair, w_cross, w_relay):
+        for copy in (ncop[2], gcop[0], gcop[2], w_pair, w_cross, w_relay):
             copy.wait_send()
         dp_all(0, 2).wait_send()
-        no_copy.wait_send()
+        output_copies('wait_send')
         dn_copy.wait_send()
         for k in range(2 * layers):
             part_copy(k).wait_send()
@@ -994,7 +1023,7 @@
                 RESULT((layers, 2, cols, D), F32), RESULT((layers, D), F32), RESULT((layers, cols, D), F32), RESULT((3, layers, cols), F32)]
         scratch = [
             *[vm(a.shape, a.dtype) for a in args[4:]], vm((wrows, D), F32), vm((3, wrows, D), F32),
-            *[vm((many, packed, D), F32) for many in (2, 3, 2, 3)], *[vm((packed, D), F32)] * 4, vm((cols, npad), F32),
+            *[vm((many, packed, D), F32) for many in (2, 3, 2, 3)], *[vm((packed, D), F32)] * 2, vm((cols, npad), F32),
             vm((2, 3, cols + cols // GROUP, D), F32), vm((4, 3, cols + cols // GROUP, D), F32), *[vm((3, nch, cols, EC), F32)] * 6,
             vm((2 * layers, D, npad), F32), vm((2 * layers, D, npad), F32),
             vm((layers, D, eh), F32), vm((layers, D, eh), F32), vm((layers, eh), F32),

time: 149 us -> 149 us (level)
  no operation moved by 1% of the time
where the time goes in v9:
time: 149 us
  Pallas kernels  148 us (99%)
    pallas_call x1, Pallas kernels, local_step(): pl.pallas_call(lambda *refs: pl.run_scoped(lambda *own: step_kernel(dims,...  146 us

profile of v9, /device:TPU:0, one launch (start us, length us, event | category | flops | bytes accessed | tf_op | source)
XLA Modules:
  0.0 148.6 jit_solution(13982769334147282039)
XLA Ops:
  0.6 146.0 %graph_step.1 = (bf16[2,32,1885]{2,1,0:T(8,128)(2,1)S(1)}, bf16[2,32,10910]{2,1,0:T(8,128)(2,1)S(1)}, bf16[2,32,1885]{2,1,0:T(8,128)(2,1)S(1)}, bf16[2,32,10910]...) custom-call(bf16[2,32,1885]{2,1,0:T(8,128)(2,1)} %bitcast.24, ...), custom_call_target="tpu_custom_call" | custom-call | tf_op jit(solution)/shard_map/graph_step/pallas_call | solution.py:1039
  146.7 1.8 %finish.1 = (bf16[2,32,1885]{2,1,0:T(8,128)(2,1)}, bf16[2,32,10910]{2,1,0:T(8,128)(2,1)}, bf16[2,32,1885]{2,1,0:T(8,128)(2,1)}, bf16[2,32,10910]{2,1,0:T(8,128)(...) custom-call(bf16[2,32,1885]{2,1,0:T(8,128)(2,1)S(1)} %get-tuple-elem, ...), custom_call_target="tpu_custom_call" | custom-call | tf_op jit(solution)/shard_map/finish/pallas_call | solution.py:982

commit v10 on v9

--- a/solution.py
+++ b/solution.py
@@ -194,13 +194,14 @@
                 remote(send.at[0], recv.at[1], n_ss.at[kind, 1], n_rs.at[kind, 1], 2),
                 remote(recv.at[1], recv.at[2], n_ss.at[kind, 2], n_rs.at[kind, 2], 1))
 
-    piece = w_send.shape[0] // dpn
+    piece = w_send.shape[0] // (dpn - 1)
+    brings = p > 0
 
     def packed(l, k, count=1):
         return pl.ds(HEAD + l * LROWS + k * cols, count * cols)
 
     def weight_rows(owner):
-        return pl.ds(pl.multiple_of(owner * piece, 8), piece)
+        return pl.ds(pl.multiple_of((owner - 1) * piece, 8), piece)
 
     w_pair = remote(w_send, w_recv.at[0], w_ss.at[0], w_rs.at[0], 1)
     w_cross = remote(w_send.at[weight_rows(p)], w_recv.at[1, weight_rows(p)], w_ss.at[1], w_rs.at[1], 2)
@@ -258,7 +259,9 @@
     def edge_start(kind, j, d):
         other = oc if d % 2 else c
         if outward(kind):
-            send_sem, recv_sem = jnp.where(j == last, 1, 0), jnp.where(j == last, 2 + slot(d), jnp.where(j < hold, 0, 1))
+            at_last = j == last
+            send_sem = jnp.asarray(at_last, jnp.int32)
+            recv_sem = jnp.where(at_last, 2 + slot(d), jnp.asarray(j >= hold, jnp.int32))
         else:
             send_sem, recv_sem = jnp.where(j == last, d, 0), j
 
@@ -321,9 +324,12 @@
         return dp_remote(half.at[l, pl.ds(seat(lax.rem(p + i, dpn)) * per, per)], dp_recv.at[l, pl.ds((i - 1) * per, per)], 0, l, i)
 
     def dp_all(l, stage):
-        most = (dpn - 1) * per
-        part_of = (dp_recv.at[l], gathered.at[l, slice(most)], w_recv.at[1, slice((dpn - 1) * piece)])[stage]
+        part_of = (dp_recv.at[l], gathered.at[l, slice((dpn - 1) * per)])[stage]
         return dp_remote(part_of, part_of, stage, l, 1)
+
+    def pieces(count):
+        part_of = w_recv.at[1, slice(count * piece)]
+        return dp_remote(part_of, part_of, 2, 0, 1)
 
     def cross_copy(l):
         return remote(cross_send.at[l], cross_recv.at[l], cross_ss.at[l], cross_rs.at[l], 2)
@@ -465,7 +471,7 @@
 
             @pl.when(t == LEADER)
             def _():
-                pl.semaphore_wait(ready, 1)
+                pl.semaphore_wait(ready)
 
         first_load.wait()
         with jax.named_scope('send_nodes'):
@@ -488,7 +494,7 @@
             w_send[packed(l, 3), :] = ew2_in[pl.ds(l * q, q), :].astype(F32)
             w_send[packed(l, 4, 2), :] = nw1_in[pl.ds(l * 2 * q, 2 * q), :].astype(F32)
             w_send[packed(l, 6), :] = nw2_in[pl.ds(l * q, q), :].astype(F32)
-        w_cross.start()
+        pl.when(brings)(w_cross.start)
         w_pair.start()
         edge_load.wait()
         with jax.named_scope('send_edges'):
@@ -515,11 +521,13 @@
 
             @pl.when(t != LEADER)
             def _():
-                pl.semaphore_wait(ready, 1)
-
-        w_cross.wait_recv()
-        for i in dp_others:
-            weight_copy(i, p).start()
+                pl.semaphore_wait(ready)
+
+        @pl.when(brings)
+        def _():
+            w_cross.wait_recv()
+            for i in dp_others:
+                weight_copy(i, p).start()
 
         @pl.when(c == 1)
         def _():
@@ -579,7 +587,9 @@
         for d in OTHERS:
             unpack_nodes(n_recv.at[slot(d)], put_rows(v0, rows_of(d)))
         with jax.named_scope('weight_wait'):
-            dp_all(0, 2).wait_recv()
+            pl.when(jnp.logical_not(brings))(pieces(dpn - 1).wait_recv)
+            if dpn > 2:
+                pl.when(brings)(pieces(dpn - 2).wait_recv)
             w_relay.start()
             w_pair.wait_recv()
             w_relay.wait_recv()
@@ -936,9 +946,14 @@
             cross_copy(l).wait_send()
             dp_all(l, 0).wait_send()
             dp_all(l, 1).wait_send()
-        for copy in (ncop[2], gcop[0], gcop[2], w_pair, w_cross, w_relay):
+        for copy in (ncop[2], gcop[0], gcop[2], w_pair, w_relay):
             copy.wait_send()
-        dp_all(0, 2).wait_send()
+
+        @pl.when(brings)
+        def _():
+            w_cross.wait_send()
+            pieces(dpn - 1).wait_send()
+
         output_copies('wait_send')
         dn_copy.wait_send()
         for k in range(2 * layers):
@@ -1016,7 +1031,7 @@
                 lead(edge_vec), lead(node_vec), edge_b1, node_b1)
         vm, sem = pltpu.VMEM, pltpu.SemaphoreType.DMA
         packed = nodes // D * cols + -(-(nodes % D) * GROUP // D) * cols // GROUP
-        wrows = -(-(HEAD + layers * LROWS) // (8 * dpn)) * 8 * dpn
+        wrows = -(-(HEAD + layers * LROWS) // (8 * (dpn - 1))) * 8 * (dpn - 1)
         lat_n, lat_e = (2, cols, nodes), (2, cols, edges)
         outs = [RESULT(lat_n, BF), RESULT(lat_e, BF), RESULT(lat_n, BF), RESULT(lat_e, BF),
                 RESULT((layers, 3, cols, D), F32), RESULT((layers, D), F32), RESULT((layers, cols, D), F32), RESULT((3, layers, cols), F32),
@@ -1024,7 +1039,7 @@
         scratch = [
             *[vm(a.shape, a.dtype) for a in args[4:]], vm((wrows, D), F32), vm((3, wrows, D), F32),
             *[vm((many, packed, D), F32) for many in (2, 3, 2, 3)], *[vm((packed, D), F32)] * 2, vm((cols, npad), F32),
-            vm((2, 3, cols + cols // GROUP, D), F32), vm((4, 3, cols + cols // GROUP, D), F32), *[vm((3, nch, cols, EC), F32)] * 6,
+            *[vm((kinds, len(OTHERS), cols + cols // GROUP, D), F32) for kinds in (2, GROUP)], *[vm((len(OTHERS), nch, cols, EC), F32)] * 6,
             vm((2 * layers, D, npad), F32), vm((2 * layers, D, npad), F32),
             vm((layers, D, eh), F32), vm((layers, D, eh), F32), vm((layers, eh), F32),
             vm((layers, D, npad), F32), vm((layers, D, npad), F32), vm((layers, npad), F32),

time: 149 us -> 148 us (level)
  no operation moved by 1% of the time
where the time goes in v10:
time: 148 us
  Pallas kernels  147 us (99%)
    pallas_call x1, Pallas kernels, local_step(): pl.pallas_call(lambda *refs: pl.run_scoped(lambda *own: step_kernel(dims,...  145 us

profile of v10, /device:TPU:0, one launch (start us, length us, event | category | flops | bytes accessed | tf_op | source)
XLA Modules:
  0.0 147.9 jit_solution(6742298819851616004)
XLA Ops:
  0.6 145.3 %graph_step.1 = (bf16[2,32,1885]{2,1,0:T(8,128)(2,1)S(1)}, bf16[2,32,10910]{2,1,0:T(8,128)(2,1)S(1)}, bf16[2,32,1885]{2,1,0:T(8,128)(2,1)S(1)}, bf16[2,32,10910]...) custom-call(bf16[2,32,1885]{2,1,0:T(8,128)(2,1)} %bitcast.24, ...), custom_call_target="tpu_custom_call" | custom-call | tf_op jit(solution)/shard_map/graph_step/pallas_call | solution.py:1054
  146.0 1.8 %finish.1 = (bf16[2,32,1885]{2,1,0:T(8,128)(2,1)}, bf16[2,32,10910]{2,1,0:T(8,128)(2,1)}, bf16[2,32,1885]{2,1,0:T(8,128)(2,1)}, bf16[2,32,10910]{2,1,0:T(8,128)(...) custom-call(bf16[2,32,1885]{2,1,0:T(8,128)(2,1)S(1)} %get-tuple-elem, ...), custom_call_target="tpu_custom_call" | custom-call | tf_op jit(solution)/shard_map/finish/pallas_call | solution.py:997

commit v11 on v10

--- a/solution.py
+++ b/solution.py
@@ -10,7 +10,7 @@
 T = 256
 TN = 384
 EC = 512
-KS = 1408
+KS = 2816
 BF = jnp.bfloat16
 F32 = jnp.float32
 I16 = jnp.int16
@@ -166,7 +166,7 @@
     n_out = 12
     (node_raw, edge_raw, gnode_raw, gedge_raw, ew1_buf, eb1_buf, ew2_buf, evec_buf, nw1_buf, nb1_buf, nw2_buf, nvec_buf) = refs[n_in:n_in + n_out]
     (send_ids, recv_ids, ew1_in, ew2_in, nw1_in, nw2_in, evec_in, nvec_in, eb1_in, nb1_in, w_send, w_recv, n_send, n_recv, gn_send, gn_recv, no_recv, dn_recv,
-     node_pad, t_send, t_recv, e_send, g_send, e_recv, g_recv, eo_recv, de_recv, part, part_recv, hidden, normed, inv, nhid, nnrm, ninv, d_part, s_sum, r_sum,
+     node_pad, t_send, t_recv, e_send, g_send, e_recv, g_recv, eo_recv, de_recv, part, part_recv, hidden, normed, inv, nhid, nnrm, ninv, d_part,
      ids_raw, bias_cols, sums, grad, core_recv, half, dp_recv, cross_send, cross_recv, own_sum, gathered,
      core_rs, dp_rs, cross_rs, w_rs, n_rs, e_rs, o_rs, p_rs, ready, load_sem, w_ss, n_ss, e_ss, p_ss, core_ss, dp_ss, cross_ss) = refs[n_in + n_out:]
 
@@ -698,6 +698,9 @@
         output_copies('start')
         node_raw[x] = tables[layers][:q, :nodes]
 
+        for k in range(layers):
+            part_copy(k).wait_send()
+        s_sum, r_sum = (part.at[k] for k in BOTH)
         grad[...] = jnp.zeros_like(grad)
         sums[...] = jnp.zeros_like(sums)
         with jax.named_scope('grad_node_wait'):
@@ -956,7 +959,7 @@
 
         output_copies('wait_send')
         dn_copy.wait_send()
-        for k in range(2 * layers):
+        for k in range(layers, 2 * layers):
             part_copy(k).wait_send()
         edges_sent(EDGE_OUT)
         with jax.named_scope('place_last'):
@@ -1043,7 +1046,7 @@
             vm((2 * layers, D, npad), F32), vm((2 * layers, D, npad), F32),
             vm((layers, D, eh), F32), vm((layers, D, eh), F32), vm((layers, eh), F32),
             vm((layers, D, npad), F32), vm((layers, D, npad), F32), vm((layers, npad), F32),
-            vm((D, npad), F32), vm((D, npad), F32), vm((D, npad), F32), vm((2, 2 * eh), jnp.int32), vm((D, D), F32), vm((layers, 2, 4 * D, D), F32),
+            vm((D, npad), F32), vm((2, 2 * eh), jnp.int32), vm((D, D), F32), vm((layers, 2, 4 * D, D), F32),
             vm((layers, SLABS, D, D), F32), vm((layers, 2, SLABS, cols, D), F32), vm((layers, SLABS, 2, cols, D), F32),
             vm((layers, (dpn - 1) * per, 2, cols, D), F32), vm((layers, per, cols, D), F32), vm((layers, per, cols, D), F32),
             vm((layers, per, cols, D), F32), vm((layers, SLABS, cols, D), F32),]

time: 148 us -> 148 us (level)
  no operation moved by 1% of the time
where the time goes in v11:
time: 148 us
  Pallas kernels  147 us (99%)
    pallas_call x1, Pallas kernels, local_step(): pl.pallas_call(lambda *refs: pl.run_scoped(lambda *own: step_kernel(dims,...  145 us

profile of v11, /device:TPU:0, one launch (start us, length us, event | category | flops | bytes accessed | tf_op | source)
XLA Modules:
  0.0 147.9 jit_solution(3479631794973514504)
XLA Ops:
  0.6 145.3 %graph_step.1 = (bf16[2,32,1885]{2,1,0:T(8,128)(2,1)S(1)}, bf16[2,32,10910]{2,1,0:T(8,128)(2,1)S(1)}, bf16[2,32,1885]{2,1,0:T(8,128)(2,1)S(1)}, bf16[2,32,10910]...) custom-call(bf16[2,32,1885]{2,1,0:T(8,128)(2,1)} %bitcast.24, ...), custom_call_target="tpu_custom_call" | custom-call | tf_op jit(solution)/shard_map/graph_step/pallas_call | solution.py:1057
  146.0 1.8 %finish.1 = (bf16[2,32,1885]{2,1,0:T(8,128)(2,1)}, bf16[2,32,10910]{2,1,0:T(8,128)(2,1)}, bf16[2,32,1885]{2,1,0:T(8,128)(2,1)}, bf16[2,32,10910]{2,1,0:T(8,128)(...) custom-call(bf16[2,32,1885]{2,1,0:T(8,128)(2,1)S(1)} %get-tuple-elem, ...), custom_call_target="tpu_custom_call" | custom-call | tf_op jit(solution)/shard_map/finish/pallas_call | solution.py:1000

commit v12 on v11

--- a/solution.py
+++ b/solution.py
@@ -25,7 +25,7 @@
 EDGE_IN, GRAD_IN, EDGE_OUT, GRAD_OUT = range(4)
 SEND_ORDER = (2, 3, 1)
 LROWS = 7 * (D // 4)
-HEAD = 16
+HEAD = 8
 LEADER = GROUP - 1
 HELPER = LEADER - 1
 VMEM_LIMIT = 63_000_000
@@ -194,21 +194,29 @@
                 remote(send.at[0], recv.at[1], n_ss.at[kind, 1], n_rs.at[kind, 1], 2),
                 remote(recv.at[1], recv.at[2], n_ss.at[kind, 2], n_rs.at[kind, 2], 1))
 
-    piece = w_send.shape[0] // (dpn - 1)
+    piece = (w_send.shape[0] - HEAD) // (dpn - 1)
     brings = p > 0
 
     def packed(l, k, count=1):
         return pl.ds(HEAD + l * LROWS + k * cols, count * cols)
 
-    def weight_rows(owner):
-        return pl.ds(pl.multiple_of((owner - 1) * piece, 8), piece)
+    def by_share(action):
+        @pl.when(brings)
+        def _():
+            action(pl.ds(pl.multiple_of(HEAD + (p - 1) * piece, HEAD), piece))
+
+        @pl.when(jnp.logical_not(brings))
+        def _():
+            action(slice(HEAD))
 
     w_pair = remote(w_send, w_recv.at[0], w_ss.at[0], w_rs.at[0], 1)
-    w_cross = remote(w_send.at[weight_rows(p)], w_recv.at[1, weight_rows(p)], w_ss.at[1], w_rs.at[1], 2)
+    def w_cross(rows):
+        return remote(w_send.at[rows], w_recv.at[1, rows], w_ss.at[1], w_rs.at[1], 2)
+
     w_relay = remote(w_recv.at[1], w_recv.at[2], w_ss.at[2], w_rs.at[2], 1)
 
-    def weight_copy(i, owner):
-        rows = w_recv.at[1, weight_rows(owner)]
+    def weight_copy(i, rows):
+        rows = w_recv.at[1, rows]
         return dp_remote(rows, rows, 2, 0, i)
 
     last = nch - 1
@@ -327,8 +335,8 @@
         part_of = (dp_recv.at[l], gathered.at[l, slice((dpn - 1) * per)])[stage]
         return dp_remote(part_of, part_of, stage, l, 1)
 
-    def pieces(count):
-        part_of = w_recv.at[1, slice(count * piece)]
+    def weight_part(rows):
+        part_of = w_recv.at[1, slice(rows)]
         return dp_remote(part_of, part_of, 2, 0, 1)
 
     def cross_copy(l):
@@ -487,14 +495,13 @@
         q = cols
         w_send[:HEAD, :] = jnp.zeros((HEAD, D), F32)
         for k in THREE:
-            w_send[k * layers:(k + 1) * layers, :cols] = evec_in[k]
-            w_send[(3 + k) * layers:(4 + k) * layers, :cols] = nvec_in[k]
+            w_send[k:k + 1, :] = beside([src[k, l:l + 1, :] for src in (evec_in, nvec_in) for l in range(layers)])
         for l in range(layers):
             w_send[packed(l, 0, 3), :] = ew1_in[pl.ds(l * 3 * q, 3 * q), :].astype(F32)
             w_send[packed(l, 3), :] = ew2_in[pl.ds(l * q, q), :].astype(F32)
             w_send[packed(l, 4, 2), :] = nw1_in[pl.ds(l * 2 * q, 2 * q), :].astype(F32)
             w_send[packed(l, 6), :] = nw2_in[pl.ds(l * q, q), :].astype(F32)
-        pl.when(brings)(w_cross.start)
+        by_share(lambda rows: w_cross(rows).start())
         w_pair.start()
         edge_load.wait()
         with jax.named_scope('send_edges'):
@@ -523,11 +530,12 @@
             def _():
                 pl.semaphore_wait(ready)
 
-        @pl.when(brings)
-        def _():
-            w_cross.wait_recv()
+        def hand_on(rows):
+            w_cross(rows).wait_recv()
             for i in dp_others:
-                weight_copy(i, p).start()
+                weight_copy(i, rows).start()
+
+        by_share(hand_on)
 
         @pl.when(c == 1)
         def _():
@@ -587,19 +595,19 @@
         for d in OTHERS:
             unpack_nodes(n_recv.at[slot(d)], put_rows(v0, rows_of(d)))
         with jax.named_scope('weight_wait'):
-            pl.when(jnp.logical_not(brings))(pieces(dpn - 1).wait_recv)
-            if dpn > 2:
-                pl.when(brings)(pieces(dpn - 2).wait_recv)
+            pl.when(jnp.logical_not(brings))(weight_part(w_send.shape[0] - HEAD).wait_recv)
+            pl.when(brings)(weight_part(w_send.shape[0] - piece).wait_recv)
             w_relay.start()
             w_pair.wait_recv()
             w_relay.wait_recv()
-        rows_all = beside([w_send[:HEAD, :cols]] + [w_recv[d, :HEAD, :cols] for d in range(3)])
-        vecs[...] = flip(stacked([rows_all, jnp.zeros((D - HEAD, D), F32)]))
+        blocks = [w_send] + [w_recv.at[d] for d in THREE]
+        rows_all = beside([stacked([src[:HEAD, rows_of(g)] for g in range(GROUP)]) for src in blocks])
+        vecs[...] = flip(stacked([rows_all, jnp.zeros((D - rows_all.shape[0], D), F32)]))
         join_weights(0)
 
         def vec(l, node):
-            first = 6 * node + l
-            return [vecs[:, first + 2 * k:first + 2 * k + 1] for k in THREE]
+            first = (node * layers + l) * HEAD
+            return [vecs[:, first + k:first + k + 1] for k in THREE]
 
         def bias(l, node):
             return bias_cols[:, node * layers + l:node * layers + l + 1]
@@ -952,10 +960,9 @@
         for copy in (ncop[2], gcop[0], gcop[2], w_pair, w_relay):
             copy.wait_send()
 
-        @pl.when(brings)
-        def _():
-            w_cross.wait_send()
-            pieces(dpn - 1).wait_send()
+        by_share(lambda rows: w_cross(rows).wait_send())
+        pl.when(brings)(weight_part((dpn - 1) * piece).wait_send)
+        pl.when(jnp.logical_not(brings))(weight_part((dpn - 1) * HEAD).wait_send)
 
         output_copies('wait_send')
         dn_copy.wait_send()
@@ -1034,7 +1041,7 @@
                 lead(edge_vec), lead(node_vec), edge_b1, node_b1)
         vm, sem = pltpu.VMEM, pltpu.SemaphoreType.DMA
         packed = nodes // D * cols + -(-(nodes % D) * GROUP // D) * cols // GROUP
-        wrows = -(-(HEAD + layers * LROWS) // (8 * (dpn - 1))) * 8 * (dpn - 1)
+        wrows = HEAD + layers * LROWS
         lat_n, lat_e = (2, cols, nodes), (2, cols, edges)
         outs = [RESULT(lat_n, BF), RESULT(lat_e, BF), RESULT(lat_n, BF), RESULT(lat_e, BF),
                 RESULT((layers, 3, cols, D), F32), RESULT((layers, D), F32), RESULT((layers, cols, D), F32), RESULT((3, layers, cols), F32),

time: 148 us -> 148 us (level)
  no operation moved by 1% of the time
where the time goes in v12:
time: 148 us
  Pallas kernels  147 us (99%)
    pallas_call x1, Pallas kernels, local_step(): pl.pallas_call(lambda *refs: pl.run_scoped(lambda *own: step_kernel(dims,...  145 us

profile of v12, /device:TPU:0, one launch (start us, length us, event | category | flops | bytes accessed | tf_op | source)
XLA Modules:
  0.0 148.0 jit_solution(14102586568766013509)
XLA Ops:
  0.6 145.4 %graph_step.1 = (bf16[2,32,1885]{2,1,0:T(8,128)(2,1)S(1)}, bf16[2,32,10910]{2,1,0:T(8,128)(2,1)S(1)}, bf16[2,32,1885]{2,1,0:T(8,128)(2,1)S(1)}, bf16[2,32,10910]...) custom-call(bf16[2,32,1885]{2,1,0:T(8,128)(2,1)} %bitcast.24, ...), custom_call_target="tpu_custom_call" | custom-call | tf_op jit(solution)/shard_map/graph_step/pallas_call | solution.py:1064
  146.0 1.8 %finish.1 = (bf16[2,32,1885]{2,1,0:T(8,128)(2,1)}, bf16[2,32,10910]{2,1,0:T(8,128)(2,1)}, bf16[2,32,1885]{2,1,0:T(8,128)(2,1)}, bf16[2,32,10910]{2,1,0:T(8,128)(...) custom-call(bf16[2,32,1885]{2,1,0:T(8,128)(2,1)S(1)} %get-tuple-elem, ...), custom_call_target="tpu_custom_call" | custom-call | tf_op jit(solution)/shard_map/finish/pallas_call | solution.py:1007

commit v13 on v12

--- a/solution.py
+++ b/solution.py
@@ -302,12 +302,15 @@
             edge_part(kind, every, (slice(0, hold), slice(hold, last))[group], False, 0, group, 1).wait_recv()
         else:
             for d in OTHERS:
-                def arrived(tail):
-                    edge_part(kind, slot(d), last, tail, 0, 2 + slot(d), d).wait_recv()
-                    if tail:
-                        unpack_tail(kind, d)
-
-                by_half(oc if d % 2 else c, last, arrived)
+                last_arrived(kind, d)
+
+    def last_arrived(kind, d):
+        def arrived(tail):
+            edge_part(kind, slot(d), last, tail, 0, 2 + slot(d), d).wait_recv()
+            if tail:
+                unpack_tail(kind, d)
+
+        by_half(oc if d % 2 else c, last, arrived)
 
     def core_copy(l, b, stage):
         return remote(grad.at[l, STAGES[stage], pl.ds((2 * b + 1) * cols, cols), :], core_recv.at[l, b, STAGES[stage]],
@@ -378,9 +381,12 @@
     def node_rows(k):
         return slice(k * cols, (k + 1) * cols) if k < tiles else pl.ds(tiles * cols + (k - tiles) * cols // GROUP, cols // GROUP)
 
-    def pack_nodes(take, out):
-        for k in range(tiles):
+    def pack_tiles(take, out, which):
+        for k in which:
             out[node_rows(k), :] = take(k * D, D)
+
+    def pack_nodes(take, out, first=0):
+        pack_tiles(take, out, range(first, tiles))
         for k, start in enumerate(over):
             val = take(start, wide)
             out[node_rows(tiles + k), :] = beside([val[r] for r in rest])
@@ -404,6 +410,14 @@
             ref[ox, :, start:start + used] = val[:, :used].astype(ref.dtype)
 
         return put
+
+    def take_raw(raw, sample):
+        def take(start, width):
+            used = min(width, nodes - start)
+            val = raw[sample, :, start:start + used].astype(F32)
+            return val if used == width else beside([val, jnp.zeros((cols, width - used), F32)])
+
+        return take
 
     def take_rows(ref, rows):
         return lambda start, width: ref[rows, start:start + width].astype(F32)
@@ -482,10 +496,17 @@
                 pl.semaphore_wait(ready)
 
         first_load.wait()
-        with jax.named_scope('send_nodes'):
-            load_nodes(node_raw, ox, n_send.at[0])
         ncop = node_copies(n_send, n_recv, 0)
-        ncop[1].start()
+        early = tiles // 2
+        take, out = take_raw(node_raw, ox), n_send.at[0]
+        pack_tiles(take, out, range(early))
+
+        def send_part(rows):
+            remote(out.at[rows], n_recv.at[1, rows], n_ss.at[0, 1], n_rs.at[0, 1], 2).start()
+
+        send_part(slice(early * cols))
+        pack_nodes(take, out, early)
+        send_part(slice(early * cols, out.shape[0]))
         node_load.wait()
         load_nodes(node_raw, x, n_send.at[1])
         keep_nodes(v0)
@@ -970,8 +991,9 @@
             part_copy(k).wait_send()
         edges_sent(EDGE_OUT)
         with jax.named_scope('place_last'):
-            group_arrived(GRAD_OUT, 2)
-            loop(nch, place_g, last)
+            for d in (1, 2, 3):
+                last_arrived(GRAD_OUT, d)
+                place_edges(gedge_raw, de_recv[slot(d), last], d, last)
         edges_sent(GRAD_OUT)
 
     bf = lambda *s: pltpu.VMEM(s, BF)

time: 148 us -> 148 us (level)
  no operation moved by 1% of the time
where the time goes in v13:
time: 148 us
  Pallas kernels  147 us (99%)
    pallas_call x1, Pallas kernels, local_step(): pl.pallas_call(lambda *refs: pl.run_scoped(lambda *own: step_kernel(dims,...  145 us

profile of v13, /device:TPU:0, one launch (start us, length us, event | category | flops | bytes accessed | tf_op | source)
XLA Modules:
  0.0 147.9 jit_solution(8955996491194935428)
XLA Ops:
  0.6 145.3 %graph_step.1 = (bf16[2,32,1885]{2,1,0:T(8,128)(2,1)S(1)}, bf16[2,32,10910]{2,1,0:T(8,128)(2,1)S(1)}, bf16[2,32,1885]{2,1,0:T(8,128)(2,1)S(1)}, bf16[2,32,10910]...) custom-call(bf16[2,32,1885]{2,1,0:T(8,128)(2,1)} %bitcast.24, ...), custom_call_target="tpu_custom_call" | custom-call | tf_op jit(solution)/shard_map/graph_step/pallas_call | solution.py:1086
  145.9 1.8 %finish.1 = (bf16[2,32,1885]{2,1,0:T(8,128)(2,1)}, bf16[2,32,10910]{2,1,0:T(8,128)(2,1)}, bf16[2,32,1885]{2,1,0:T(8,128)(2,1)}, bf16[2,32,10910]{2,1,0:T(8,128)(...) custom-call(bf16[2,32,1885]{2,1,0:T(8,128)(2,1)S(1)} %get-tuple-elem, ...), custom_call_target="tpu_custom_call" | custom-call | tf_op jit(solution)/shard_map/finish/pallas_call | solution.py:1029

commit v14 on v13

--- a/solution.py
+++ b/solution.py
@@ -497,7 +497,7 @@
 
         first_load.wait()
         ncop = node_copies(n_send, n_recv, 0)
-        early = tiles // 2
+        early = 2
         take, out = take_raw(node_raw, ox), n_send.at[0]
         pack_tiles(take, out, range(early))
 

time: 148 us -> 148 us (level)
  no operation moved by 1% of the time
where the time goes in v14:
time: 148 us
  Pallas kernels  147 us (99%)
    pallas_call x1, Pallas kernels, local_step(): pl.pallas_call(lambda *refs: pl.run_scoped(lambda *own: step_kernel(dims,...  145 us

profile of v14, /device:TPU:0, one launch (start us, length us, event | category | flops | bytes accessed | tf_op | source)
XLA Modules:
  0.0 147.9 jit_solution(2170534260136711090)
XLA Ops:
  0.6 145.3 %graph_step.1 = (bf16[2,32,1885]{2,1,0:T(8,128)(2,1)S(1)}, bf16[2,32,10910]{2,1,0:T(8,128)(2,1)S(1)}, bf16[2,32,1885]{2,1,0:T(8,128)(2,1)S(1)}, bf16[2,32,10910]...) custom-call(bf16[2,32,1885]{2,1,0:T(8,128)(2,1)} %bitcast.24, ...), custom_call_target="tpu_custom_call" | custom-call | tf_op jit(solution)/shard_map/graph_step/pallas_call | solution.py:1086
  145.9 1.8 %finish.1 = (bf16[2,32,1885]{2,1,0:T(8,128)(2,1)}, bf16[2,32,10910]{2,1,0:T(8,128)(2,1)}, bf16[2,32,1885]{2,1,0:T(8,128)(2,1)}, bf16[2,32,10910]{2,1,0:T(8,128)(...) custom-call(bf16[2,32,1885]{2,1,0:T(8,128)(2,1)S(1)} %get-tuple-elem, ...), custom_call_target="tpu_custom_call" | custom-call | tf_op jit(solution)/shard_map/finish/pallas_call | solution.py:1029
